TPU v7x, 32 devices: a whole 2x2x4 slice. The times are simulated.
32 devices in a mesh: tok: 2 (over x), blk: 16 (over z, y, core).
Axes of the slice: x: 2, y: 2, z: 4, core: 2. Of those that a mesh axis runs over, the one named last changes fastest.
Arguments:
- grad_out: bfloat16 [2048, 8192], P('tok', 'blk'), may hold values from -6 to 6
- acts: bfloat16 [2048, 512], P('tok', 'blk'), may hold values from -6 to 6
- stat_old: float32 [2, 16, 512, 512], P('tok', 'blk'), may hold values from -1 to 6, as said below
- root_old: float32 [2, 16, 512, 512], P('tok', 'blk'), may hold values from -1 to 2, as said below
- assign: int32 [16, 2], P('blk'), may hold values from 0 to 1, as said below
Outputs:
- roots: float32 [2, 16, 512, 512], P('tok', 'blk')
- precond: float32 [2, 16, 256, 512], P('tok', 'blk')
Inputs may be any that keep to these rules, and one draw needn't show every extreme that they name: `assign`: row j gives each of its 2 slots a job 2 b + s with b < 1 and s in 0, 1; every job once in a row; slots 2 m and 2 m + 1 hold the two sides of one block. `stat_old`: each slot's matrix is symmetric and positive definite. `root_old`: each slot's matrix is symmetric.
All inputs are finite; a program needn't handle non-finite values.
Results may differ from a plain program's by a relative error of at most 0.0003.
Values may be sent and summed in bfloat16 or wider, within the bound.
No kernel may reach another device: no remote copies, remote signals or barrier semaphores. Data moves between devices by JAX's collectives and lax.ppermute only.
A program may use at most 64 MiB of HBM per device.

v0:
```python
import functools
import math

import jax
import jax.numpy as jnp
from jax import lax
from jax.experimental import pallas as pl
from jax.experimental.pallas import tpu as pltpu
from jax.sharding import PartitionSpec as P


ITERS = 2


BETA = 0.9
DAMPING = 0.001
TAIL = 8
GRANT = 24 << 20


def swapped(block, axis, stride):
    return moved(block, axis, 1 << stride)


def crossed(block, mask):
    half = lax.axis_size("blk")
    return lax.ppermute(
        block, ("tok", "blk"), [(low, low ^ half ^ mask) for low in range(2 * half)]
    )


def moved(block, axis, mask):
    count = lax.axis_size(axis)
    return lax.ppermute(block, axis, [(low, low ^ mask) for low in range(count) if low ^ mask < count])


def product(lhs_matrix, rhs_matrix):
    return jnp.dot(
        lhs_matrix, rhs_matrix, precision=lax.Precision.HIGH, preferred_element_type=jnp.float32
    )


def newton_root(statistic, warm_root, square):
    identity = jnp.eye(square.shape[0], dtype=jnp.float32)
    factor = BETA * statistic + (1.0 - BETA) * square + DAMPING * identity
    root_square = product(warm_root, warm_root)
    coupled = product(product(root_square, root_square), factor)
    current = warm_root
    for iteration in range(ITERS):
        update = (5.0 * identity - coupled) * 0.25
        current = product(current, update)
        if iteration + 1 < ITERS:
            update_square = product(update, update)
            coupled = product(product(update_square, update_square), coupled)
    return current


def block_partials(rows_part, cols_part, group_blocks, block_size, scaling):
    shaped = cols_part.reshape(cols_part.shape[0], group_blocks, block_size)
    return (
        jnp.einsum("tr,tgc->grc", rows_part, shaped, preferred_element_type=jnp.float32) * scaling
    )


def join_pair(mine, theirs, column, bit):
    lower = column // (1 << bit) % 2 == 0
    return jnp.where(
        lower, jnp.concatenate([mine, theirs], axis=1), jnp.concatenate([theirs, mine], axis=1)
    )


def general(grad_out, acts, stat_old, root_old, assign):
    token_groups = lax.axis_size("tok")
    blk_count = lax.axis_size("blk")
    column = lax.axis_index("blk")
    position = lax.axis_index("tok")
    block_size = stat_old.shape[-1]
    shard_rows = grad_out.shape[0]
    all_tokens = shard_rows * token_groups
    scaling = 1.0 / math.sqrt(all_tokens)
    strips = grad_out.shape[1] * blk_count // block_size
    strip_bits = strips.bit_length() - 1
    blk_bits = blk_count.bit_length() - 1
    group_blocks = token_groups // 2
    cols_part = acts
    for bit in range(strip_bits):
        other_cols = swapped(cols_part, "blk", bit)
        cols_part = join_pair(cols_part, other_cols, column, bit)
    rows_part = grad_out
    for bit in range(strip_bits, blk_bits):
        other_rows = swapped(rows_part, "blk", bit)
        rows_part = join_pair(rows_part, other_rows, column, bit)
    job_table = assign[0]
    job_index = job_table[position]
    side_bit = job_index % 2
    partial_value = block_partials(rows_part, cols_part, group_blocks, block_size, scaling)
    halves = partial_value.reshape(group_blocks * 2, block_size // 2, block_size)[job_table]
    own_half = lax.psum_scatter(halves, "tok", scatter_dimension=0, tiled=True)[0]
    other_half = swapped(own_half, "tok", 0)
    chosen = jnp.where(
        side_bit == 0,
        jnp.concatenate([own_half, other_half], axis=0),
        jnp.concatenate([other_half, own_half], axis=0),
    )
    oriented = jnp.where(side_bit == 0, chosen, chosen.T)
    square = product(oriented, oriented.T) / all_tokens
    own_root = newton_root(stat_old[0, 0], root_old[0, 0], square)
    other_root = swapped(own_root, "tok", 0)
    left_root = jnp.where(side_bit == 0, own_root, other_root)
    right_root = jnp.where(side_bit == 0, other_root, own_root)
    half_rows = lax.dynamic_slice_in_dim(
        left_root, side_bit * (block_size // 2), block_size // 2, 0
    )
    precond = product(product(half_rows, chosen), right_root)
    return (own_root[None, None], precond[None, None])


def split(value):
    high = value.astype(jnp.bfloat16)
    return high, (value - high.astype(jnp.float32)).astype(jnp.bfloat16)


def multiply(lhs, rhs, dims=((1,), (0,))):
    def one(a, b):
        return lax.dot_general(a, b, (dims, ((), ())), preferred_element_type=jnp.float32)

    return one(lhs[0], rhs[0]) + (one(lhs[0], rhs[1]) + one(lhs[1], rhs[0]))


def exponent_of(value):
    largest = jnp.max(jnp.abs(value), axis=0, keepdims=True)
    return jnp.clip(jnp.ceil(jnp.log2(jnp.maximum(largest, 1e-30))), -100.0, 100.0)


def side_of(assign_ref):
    return assign_ref[0, lax.axis_index("tok")] % 2


def eye_mask(rows, cols):
    return lax.broadcasted_iota(jnp.int32, (rows, cols), 0) == lax.broadcasted_iota(
        jnp.int32, (rows, cols), 1
    )


def partial_body(*refs, scaling, pieces):
    grad_refs = refs[pieces : pieces + 2]
    outs = refs[pieces + 2 :]
    held_ref = outs[-1]
    part_rows = refs[0].shape[0]
    rows = pieces * part_rows
    for index in range(pieces):
        held_ref[index * part_rows : (index + 1) * part_rows, :] = refs[index][...]
    for which, grad_ref in enumerate(grad_refs):
        own_ref, pay_ref = outs[2 * which : 2 * which + 2]
        own = jnp.dot(held_ref[...], grad_ref[...], preferred_element_type=jnp.float32) * scaling
        own_ref[...] = own
        power = exponent_of(own)
        pay_ref[0:rows, :] = own * jnp.exp2(-power)
        pay_ref[rows:, :] = jnp.broadcast_to(power, (TAIL, own.shape[1]))


def partial_chunk(parts, grads, scaling):
    rows = sum(part.shape[0] for part in parts)
    width = grads[0].shape[1]
    return call(
        functools.partial(partial_body, scaling=scaling, pieces=len(parts)),
        [((rows, width), jnp.float32), ((rows + TAIL, width), jnp.float32)] * 2,
        [*parts, *grads],
        [pltpu.VMEM((rows, grads[0].shape[0]), grads[0].dtype)],
    )


def stage_body(*refs):
    count = len(refs) // 2
    copies = [
        pltpu.make_async_copy(refs[index], refs[count + index], refs[-1].at[index])
        for index in range(count)
    ]
    for copy in copies:
        copy.start()
    for copy in copies:
        copy.wait()


def stage(operands):
    operands = [pltpu.with_memory_space_constraint(operand, pltpu.HBM) for operand in operands]
    return pl.pallas_call(
        stage_body,
        out_shape=tuple(pltpu.VMEM(operand.shape, operand.dtype) for operand in operands),
        in_specs=[pl.BlockSpec(memory_space=pl.ANY) for _ in operands],
        out_specs=tuple(pl.BlockSpec(memory_space=pltpu.VMEM) for _ in operands),
        scratch_shapes=[pltpu.SemaphoreType.DMA((len(operands),))],
        name="stage",
        compiler_params=pltpu.CompilerParams(vmem_limit_bytes=GRANT),
    )(*operands)


def squared_body(root_ref, out_ref):
    value = split(root_ref[...])
    out_ref[...] = multiply(value, value)


def root_body(*refs, groups, all_tokens):
    assign_ref = refs[0]
    count = len(groups)
    stat_ref, warm_ref, fourth_ref = refs[1 + 2 * count : 4 + 2 * count]
    root_ref, pay_ref, high_ref, low_ref, held_ref = refs[4 + 2 * count :]
    column, side = lax.axis_index("blk"), side_of(assign_ref)
    size = stat_ref.shape[-1]
    for group, masks in enumerate(groups):
        own_ref, got_ref = refs[1 + 2 * group : 3 + 2 * group]
        rows = own_ref.shape[0]
        part_rows = rows // len(masks)
        scale = jnp.exp2(got_ref[rows : rows + 1, :])
        for index, mask in enumerate(masks):
            span = slice(index * part_rows, (index + 1) * part_rows)
            target = pl.multiple_of((column ^ mask) * part_rows, part_rows)
            held_ref[pl.ds(target, part_rows), :] = own_ref[span, :] + got_ref[span, :] * scale

    @pl.when(side == 0)
    def _():
        held_ref[...] = held_ref[...].T

    oriented = split(held_ref[...])
    high_ref[...] = oriented[0]
    low_ref[...] = oriented[1]
    square = multiply(oriented, oriented, ((1,), (1,))) * (1.0 / all_tokens)
    identity = jnp.where(eye_mask(size, size), 1.0, 0.0)
    factor = BETA * stat_ref[...] + (1.0 - BETA) * square + DAMPING * identity
    coupled = multiply(split(fourth_ref[...]), split(factor))
    current = warm_ref[...]
    for iteration in range(ITERS):
        update = split((5.0 * identity - coupled) * 0.25)
        current = multiply(split(current), update)
        if iteration + 1 < ITERS:
            update_square = split(multiply(update, update))
            coupled = multiply(split(multiply(update_square, update_square)), split(coupled))
    root_ref[...] = current
    power = exponent_of(current)
    scaled = current * jnp.exp2(-power)
    diagonal = jnp.sum(scaled * identity, axis=0, keepdims=True)
    coarse = jnp.round(diagonal * 1024.0) * (1.0 / 1024.0)
    pay_ref[0:size, :] = scaled * (1.0 - identity)
    row = lax.broadcasted_iota(jnp.int32, (TAIL, size), 0)
    tail = jnp.where(row == 0, power, jnp.where(row == 1, coarse, diagonal - coarse))
    pay_ref[size:, :] = tail


def middle_body(assign_ref, root_ref, high_ref, low_ref, out_ref):
    half = root_ref.shape[0] // 2
    oriented = high_ref[...], low_ref[...]

    @pl.when(side_of(assign_ref) == 0)
    def _():
        out_ref[0:half, :] = multiply(split(root_ref[0:half, :]), oriented)
        out_ref[half:, :] = jnp.zeros((half, root_ref.shape[1]), jnp.float32)

    @pl.when(side_of(assign_ref) != 0)
    def _():
        out_ref[...] = multiply(oriented, split(root_ref[...]), ((0,), (0,)))


def final_body(assign_ref, got_ref, middle_ref, out_ref):
    size = middle_ref.shape[0]
    half = size // 2
    scale = jnp.exp2(got_ref[size : size + 1, :])
    diagonal = got_ref[size + 1 : size + 2, :] + got_ref[size + 2 : size + 3, :]
    other = jnp.where(eye_mask(size, size), diagonal, got_ref[0:size, :]) * scale

    @pl.when(side_of(assign_ref) == 0)
    def _():
        out_ref[...] = multiply(split(middle_ref[0:half, :]), split(other))

    @pl.when(side_of(assign_ref) != 0)
    def _():
        out_ref[...] = multiply(split(other[half:, :]), split(middle_ref[...]))


def call(body, shapes, operands, scratch=()):
    smem = pl.BlockSpec(memory_space=pltpu.SMEM)
    vmem = pl.BlockSpec(memory_space=pltpu.VMEM)
    whole = [operand.dtype == jnp.int32 for operand in operands]
    operands = [
        operand if scalar else pltpu.with_memory_space_constraint(operand, pltpu.VMEM)
        for operand, scalar in zip(operands, whole)
    ]
    return pl.pallas_call(
        body,
        out_shape=tuple(pltpu.VMEM(*shape) for shape in shapes),
        in_specs=[smem if scalar else vmem for scalar in whole],
        out_specs=tuple(vmem for _ in shapes),
        scratch_shapes=list(scratch),
        compiler_params=pltpu.CompilerParams(vmem_limit_bytes=GRANT),
    )(*operands)


def paired(grad_out, acts, stat_old, root_old, assign):
    blk_count = lax.axis_size("blk")
    size = stat_old.shape[-1]
    all_tokens = grad_out.shape[0] * lax.axis_size("tok")
    scaling = 1.0 / math.sqrt(all_tokens)
    square = (size, size)
    far = [mask for mask in range(4, blk_count, 4)]
    sent = acts.T
    parts = {}
    for mask in reversed([2] + far):
        parts[mask] = moved(sent, "blk", mask)
    parts[0], grad, warm, stat = stage([sent, grad_out, root_old[0, 0], stat_old[0, 0]])
    for mask in far:
        parts[mask | 2] = moved(parts[mask], "blk", 2)
    grads = [grad, moved(grad_out, "blk", 1)]
    (second,) = call(squared_body, [(square, jnp.float32)], [warm])
    (fourth,) = call(squared_body, [(square, jnp.float32)], [second])
    groups = []
    operands = [assign]
    for masks in ([0, 2] + far[:1], far[1:], [mask | 2 for mask in far]):
        own, own_pay, beside, beside_pay = partial_chunk(
            [parts[mask] for mask in masks], grads, scaling
        )
        own_pay, beside_pay = own_pay.astype(jnp.float16), beside_pay.astype(jnp.float16)
        got, got_beside = crossed(own_pay, 0), crossed(beside_pay, 1)
        beside = moved(beside, "blk", 1)
        operands += [own, got.astype(jnp.float32), beside, got_beside.astype(jnp.float32)]
        groups += [masks, [mask | 1 for mask in masks]]
    own_root, pay, high, low = call(
        functools.partial(root_body, groups=groups, all_tokens=all_tokens),
        [
            (square, jnp.float32),
            ((size + TAIL, size), jnp.float32),
            (square, jnp.bfloat16),
            (square, jnp.bfloat16),
        ],
        operands + [stat, warm, fourth],
        [pltpu.VMEM(square, jnp.float32)],
    )
    got = moved(pay.astype(jnp.float16), "tok", 1).astype(jnp.float32)
    (middle,) = call(middle_body, [(square, jnp.float32)], [assign, own_root, high, low])
    (precond,) = call(final_body, [((size // 2, size), jnp.float32)], [assign, got, middle])
    return (own_root[None, None], precond[None, None])


def is_paired(mesh_shape, rows, size, features):
    strips = rows // size
    plain = mesh_shape["tok"] == 2 and strips == mesh_shape["blk"] and strips % 8 == 0
    return plain and features % (32 * strips) == 0


def solution(mesh):
    placed = (
        P("tok", "blk"),
        P("tok", "blk"),
        P("tok", "blk", None, None),
        P("tok", "blk", None, None),
        P("blk", None),
    )

    def whole(grad_out, acts, stat_old, root_old, assign):
        fast = is_paired(mesh.shape, grad_out.shape[1], stat_old.shape[-1], acts.shape[1])

        def shards(*args):
            return (paired if fast else general)(*args)

        mapped = jax.shard_map(
            shards,
            mesh=mesh,
            in_specs=placed,
            out_specs=(P("tok", "blk", None, None), P("tok", "blk", None, None)),
            check_vma=False,
        )
        return mapped(grad_out, acts, stat_old, root_old, assign)

    return whole
```

profile of v0, /device:TPU:0, one launch (start us, length us, event | category | flops | bytes accessed | tf_op | source)
XLA Modules:
  0.0 59.4 jit_solution(17707152169110080264)
XLA Ops:
  0.6 0.6 collective-permute-start.2
  1.2 4.7 %collective-permute-start.7 = (bf16[32,1024]{1,0:T(8,128)(2,1)}, bf16[32,1024]{1,0:T(8,128)(2,1)S(1)}, u32[]{:S(2)}, u32[]{:S(2)}) collective-permute-start(bf16[32,1024]{1,0:T(8,128)(2,1)} %bitcast.9), channel_id=1, source_target_pairs={{0,12},{1,13},{2,14},{3,15},{4,8},{5,9},{6,10},{7,11},{8,4},{9,5},... | collective-permute-start | bytes 196616 | tf_op jit(solution)/shard_map/ppermute | solution.py:34
  5.9 0.0 collective-permute-start.6
  5.9 0.6 %collective-permute-start.1 = (bf16[32,1024]{1,0:T(8,128)(2,1)}, bf16[32,1024]{1,0:T(8,128)(2,1)S(1)}, u32[]{:S(2)}, u32[]{:S(2)}) collective-permute-start(bf16[32,1024]{1,0:T(8,128)(2,1)} %bitcast.11), channel_id=1, source_target_pairs={{0,4},{1,5},{2,6},{3,7},{4,0},{5,1},{6,2},{7,3},{8,12},{9,13},{10,... | collective-permute-start | bytes 196616 | tf_op jit(solution)/shard_map/ppermute | solution.py:34
  6.5 2.5 %collective-permute-done.7.refs_1_ = bf16[32,1024]{1,0:T(8,128)(2,1)S(1)} collective-permute-done((bf16[32,1024]{1,0:T(8,128)(2,1)}, bf16[32,1024]{1,0:T(8,128)(2,1)S(1)}, u32[]{:S(2)}, u32[]{:S(2)}) %collective-permute-start.7) | collective-permute-done | bytes 65568 | tf_op jit(solution)/shard_map/ppermute | solution.py:34
  9.0 1.5 %collective-permute-start.13 = (bf16[32,1024]{1,0:T(8,128)(2,1)S(1)}, bf16[32,1024]{1,0:T(8,128)(2,1)S(1)}, u32[]{:S(2)}, u32[]{:S(2)}) collective-permute-start(bf16[32,1024]{1,0:T(8,128)(2,1)S(1)} %collective-permute-done.7.refs_1_), channel_id=1, source_target_pairs={{0,2},{1,3},{2,0},{3,1},{4,6},{5,7},{6,4},{7,5},{8,10},{9,11},{10,... | collective-permute-start | bytes 196616 | tf_op jit(solution)/shard_map/ppermute | solution.py:34
  10.5 1.6 %collective-permute-done.6.refs_0_ = bf16[32,1024]{1,0:T(8,128)(2,1)S(1)} collective-permute-done((bf16[32,1024]{1,0:T(8,128)(2,1)}, bf16[32,1024]{1,0:T(8,128)(2,1)S(1)}, u32[]{:S(2)}, u32[]{:S(2)}) %collective-permute-start.6) | collective-permute-done | bytes 65568 | tf_op jit(solution)/shard_map/ppermute | solution.py:34
  12.1 1.5 %collective-permute-start.12 = (bf16[32,1024]{1,0:T(8,128)(2,1)S(1)}, bf16[32,1024]{1,0:T(8,128)(2,1)S(1)}, u32[]{:S(2)}, u32[]{:S(2)}) collective-permute-start(bf16[32,1024]{1,0:T(8,128)(2,1)S(1)} %collective-permute-done.6.refs_0_), channel_id=1, source_target_pairs={{0,2},{1,3},{2,0},{3,1},{4,6},{5,7},{6,4},{7,5},{8,10},{9,11},{10,... | collective-permute-start | bytes 196616 | tf_op jit(solution)/shard_map/ppermute | solution.py:34
  13.6 0.0 collective-permute-done.1.refs_2_
  13.6 0.5 collective-permute-start.11
  14.1 1.9 %stage.1 = (bf16[32,1024]{1,0:T(8,128)(2,1)S(1)}, bf16[1024,512]{1,0:T(8,128)(2,1)S(1)}, f32[512,512]{1,0:T(8,128)S(1)}, f32[512,512]{1,0:T(8,128)S(1)}) custom-call(bf16[32,1024]{1,0:T(8,128)(2,1)} %bitcast.12, bf16[1024,512]{1,0:T(8,128)(2,1)} %refs_1_.1, f32[512,512]{1,0:T(8,128)} %bitcast.7, f32[512,512]{1,0:T(8,128)} %bitcast.8), custom_call_target="tpu_custom_call" | custom-call | tf_op jit(solution)/shard_map/stage/pallas_call | solution.py:187
  16.1 0.0 collective-permute-done.2.refs_4_.refs_3_
  16.1 0.0 copy-start.1
  16.1 0.5 shard_map.69
  16.6 0.3 collective-permute-start.10
  16.9 0.0 copy-done.1
  16.9 1.5 %collective-permute-start = (bf16[32,1024]{1,0:T(8,128)(2,1)S(1)}, bf16[32,1024]{1,0:T(8,128)(2,1)S(1)}, u32[]{:S(2)}, u32[]{:S(2)}) collective-permute-start(bf16[32,1024]{1,0:T(8,128)(2,1)S(1)} %bitcast.13), channel_id=1, source_target_pairs={{0,2},{1,3},{2,0},{3,1},{4,6},{5,7},{6,4},{7,5},{8,10},{9,11},{10,... | collective-permute-start | bytes 196616 | tf_op jit(solution)/shard_map/ppermute | solution.py:34
  18.5 0.0 collective-permute-done.13.refs_2_
  18.5 0.0 collective-permute-done.12.refs_1_
  18.5 0.0 collective-permute-done.11.refs_0_
  18.5 0.5 shard_map.70
  19.0 1.3 %collective-permute-start.16 = (f16[104,512]{1,0:T(8,128)(2,1)S(1)}, f16[104,512]{1,0:T(8,128)(2,1)S(1)}, u32[]{:S(2)}, u32[]{:S(2)}) collective-permute-start(f16[104,512]{1,0:T(8,128)(2,1)S(1)} %convert_element_type.52), channel_id=1, source_target_pairs={{0,17},{1,16},{2,19},{3,18},{4,21},{5,20},{6,23},{7,22},{8,25},{9,... | collective-permute-start | bytes 319496 | tf_op jit(solution)/shard_map/ppermute | solution.py:27
  20.3 1.6 %collective-permute-start.14 = (f16[104,512]{1,0:T(8,128)(2,1)S(1)}, f16[104,512]{1,0:T(8,128)(2,1)S(1)}, u32[]{:S(2)}, u32[]{:S(2)}) collective-permute-start(f16[104,512]{1,0:T(8,128)(2,1)S(1)} %convert_element_type.50), channel_id=1, source_target_pairs={{0,16},{1,17},{2,18},{3,19},{4,20},{5,21},{6,22},{7,23},{8,24},{9,... | collective-permute-start | bytes 319496 | tf_op jit(solution)/shard_map/ppermute | solution.py:27
  21.9 0.6 %collective-permute-start.8 = (f16[72,512]{1,0:T(8,128)(2,1)S(1)}, f16[72,512]{1,0:T(8,128)(2,1)S(1)}, u32[]{:S(2)}, u32[]{:S(2)}) collective-permute-start(f16[72,512]{1,0:T(8,128)(2,1)S(1)} %convert_element_type.46), channel_id=1, source_target_pairs={{0,16},{1,17},{2,18},{3,19},{4,20},{5,21},{6,22},{7,23},{8,24},{9,... | collective-permute-start | bytes 221192 | tf_op jit(solution)/shard_map/ppermute | solution.py:27
  22.5 0.0 collective-permute-done.refs_1_
  22.5 0.5 shard_map.68
  23.0 0.1 collective-permute-start.4
  23.1 0.0 collective-permute-done.10
  23.1 0.5 collective-permute-start.15
  23.6 4.7 %collective-permute-done.8 = f16[72,512]{1,0:T(8,128)(2,1)S(1)} collective-permute-done((f16[72,512]{1,0:T(8,128)(2,1)S(1)}, f16[72,512]{1,0:T(8,128)(2,1)S(1)}, u32[]{:S(2)}, u32[]{:S(2)}) %collective-permute-start.8) | collective-permute-done | bytes 73760 | tf_op jit(solution)/shard_map/ppermute | solution.py:27
  28.4 1.5 %collective-permute-start.5 = (f16[104,512]{1,0:T(8,128)(2,1)S(1)}, f16[104,512]{1,0:T(8,128)(2,1)S(1)}, u32[]{:S(2)}, u32[]{:S(2)}) collective-permute-start(f16[104,512]{1,0:T(8,128)(2,1)S(1)} %convert_element_type.44), channel_id=1, source_target_pairs={{0,17},{1,16},{2,19},{3,18},{4,21},{5,20},{6,23},{7,22},{8,25},{9,... | collective-permute-start | bytes 319496 | tf_op jit(solution)/shard_map/ppermute | solution.py:27
  29.9 0.7 %collective-permute-start.3 = (f16[104,512]{1,0:T(8,128)(2,1)S(1)}, f16[104,512]{1,0:T(8,128)(2,1)S(1)}, u32[]{:S(2)}, u32[]{:S(2)}) collective-permute-start(f16[104,512]{1,0:T(8,128)(2,1)S(1)} %convert_element_type.42), channel_id=1, source_target_pairs={{0,16},{1,17},{2,18},{3,19},{4,20},{5,21},{6,22},{7,23},{8,24},{9,... | collective-permute-start | bytes 319496 | tf_op jit(solution)/shard_map/ppermute | solution.py:27
  30.6 1.0 %shard_map.71.root_ref = f32[512,512]{1,0:T(8,128)S(1)} custom-call(f32[512,512]{1,0:T(8,128)S(1)} %get-tuple-element.37.root_ref.refs_14_), custom_call_target="tpu_custom_call" | custom-call | tf_op jit(solution)/shard_map/pallas_call | solution.py:287
  31.6 1.0 %shard_map.72.refs_15_ = f32[512,512]{1,0:T(8,128)S(1)} custom-call(f32[512,512]{1,0:T(8,128)S(1)} %shard_map.71.root_ref), custom_call_target="tpu_custom_call" | custom-call | tf_op jit(solution)/shard_map/pallas_call | solution.py:287
  32.6 0.0 copy-start
  32.7 0.6 %collective-permute-done.5 = f16[104,512]{1,0:T(8,128)(2,1)S(1)} collective-permute-done((f16[104,512]{1,0:T(8,128)(2,1)S(1)}, f16[104,512]{1,0:T(8,128)(2,1)S(1)}, u32[]{:S(2)}, u32[]{:S(2)}) %collective-permute-start.5) | collective-permute-done | bytes 106528 | tf_op jit(solution)/shard_map/ppermute | solution.py:27
  33.3 2.7 %collective-permute-done.3 = f16[104,512]{1,0:T(8,128)(2,1)S(1)} collective-permute-done((f16[104,512]{1,0:T(8,128)(2,1)S(1)}, f16[104,512]{1,0:T(8,128)(2,1)S(1)}, u32[]{:S(2)}, u32[]{:S(2)}) %collective-permute-start.3) | collective-permute-done | bytes 106528 | tf_op jit(solution)/shard_map/ppermute | solution.py:27
  36.1 0.0 collective-permute-done.9.refs_7_
  36.1 0.0 collective-permute-done.4.refs_3_
  36.1 7.9 %shard_map.73 = (f32[512,512]{1,0:T(8,128)S(1)}, f32[520,512]{1,0:T(8,128)S(1)}, bf16[512,512]{1,0:T(8,128)(2,1)S(1)}, bf16[512,512]{1,0:T(8,128)(2,1)S(1)}) custom-call(s32[1,2]{1,0:T(1,128)S(1)} %copy-done, f32[96,512]{1,0:T(8,128)S(1)} %get-tuple-element.24.refs_1_, f32[104,512]{1,0:T(8,128)S(1)} %convert_element_type.43.refs_2_, ...), custom_call_target="tpu_custom_call" | custom-call | tf_op jit(solution)/shard_map/pallas_call | solution.py:287
  44.0 0.1 convert_element_type.54
  44.1 1.1 %collective-permute-start.17 = (f16[520,512]{1,0:T(8,128)(2,1)S(1)}, f16[520,512]{1,0:T(8,128)(2,1)S(1)}, u32[]{:S(2)}, u32[]{:S(2)}) collective-permute-start(f16[520,512]{1,0:T(8,128)(2,1)S(1)} %convert_element_type.54), channel_id=1, source_target_pairs={{0,16},{16,0},{1,17},{17,1},{2,18},{18,2},{3,19},{19,3},{4,20},{20... | collective-permute-start | bytes 1597448 | tf_op jit(solution)/shard_map/ppermute | solution.py:34
  45.2 1.0 %copy.7 = f32[1,1,512,512]{3,2,1,0:T(8,128)} copy(f32[1,1,512,512]{3,2,1,0:T(8,128)S(1)} %bitcast.5) | data formatting | bytes 2097152
  46.1 1.2 %shard_map.74.middle_ref = f32[512,512]{1,0:T(8,128)S(1)} custom-call(s32[1,2]{1,0:T(1,128)S(1)} %copy-done, f32[512,512]{1,0:T(8,128)S(1)} %get-tuple-element.38.root_ref, bf16[512,512]{1,0:T(8,128)(2,1)S(1)} %get-tuple-element.40.high_ref, bf16[512,512]{1,0:T(8,128)(2,1)S(1)} %get-tuple-element.41.low_ref), custom_call_target="tpu_custom_call" | custom-call | tf_op jit(solution)/shard_map/pallas_call | solution.py:287
  47.3 9.9 %collective-permute-done.17 = f16[520,512]{1,0:T(8,128)(2,1)S(1)} collective-permute-done((f16[520,512]{1,0:T(8,128)(2,1)S(1)}, f16[520,512]{1,0:T(8,128)(2,1)S(1)}, u32[]{:S(2)}, u32[]{:S(2)}) %collective-permute-start.17) | collective-permute-done | bytes 532512 | tf_op jit(solution)/shard_map/ppermute | solution.py:34
  57.2 0.1 convert_element_type.55.got_ref
  57.4 1.3 %shard_map.75 = f32[256,512]{1,0:T(8,128)S(1)} custom-call(s32[1,2]{1,0:T(1,128)S(1)} %copy-done, f32[520,512]{1,0:T(8,128)S(1)} %convert_element_type.55.got_ref, f32[512,512]{1,0:T(8,128)S(1)} %shard_map.74.middle_ref), custom_call_target="tpu_custom_call" | custom-call | tf_op jit(solution)/shard_map/pallas_call | solution.py:287
  58.6 0.8 %copy.8 = f32[1,1,256,512]{3,2,1,0:T(8,128)} copy(f32[1,1,256,512]{3,2,1,0:T(8,128)S(1)} %bitcast.6) | data formatting | bytes 1048576
  (17 shorter events, 0.2 us)
Async XLA Ops:
  0.6 15.5 %collective-permute-start.2 = (bf16[1024,512]{1,0:T(8,128)(2,1)}, bf16[1024,512]{1,0:T(8,128)(2,1)S(1)}, u32[]{:S(2)}, u32[]{:S(2)}) collective-permute-start(bf16[1024,512]{1,0:T(8,128)(2,1)} %refs_1_.1), channel_id=1, source_target_pairs={{0,1},{1,0},{2,3},{3,2},{4,5},{5,4},{6,7},{7,6},{8,9},{9,8},{10,11... | collective-permute-start | bytes 3145736 | tf_op jit(solution)/shard_map/ppermute | solution.py:34
  1.2 7.8 %collective-permute-start.7 = (bf16[32,1024]{1,0:T(8,128)(2,1)}, bf16[32,1024]{1,0:T(8,128)(2,1)S(1)}, u32[]{:S(2)}, u32[]{:S(2)}) collective-permute-start(bf16[32,1024]{1,0:T(8,128)(2,1)} %bitcast.9), channel_id=1, source_target_pairs={{0,12},{1,13},{2,14},{3,15},{4,8},{5,9},{6,10},{7,11},{8,4},{9,5},... | collective-permute-start | bytes 196616 | tf_op jit(solution)/shard_map/ppermute | solution.py:34
  5.9 6.3 %collective-permute-start.6 = (bf16[32,1024]{1,0:T(8,128)(2,1)}, bf16[32,1024]{1,0:T(8,128)(2,1)S(1)}, u32[]{:S(2)}, u32[]{:S(2)}) collective-permute-start(bf16[32,1024]{1,0:T(8,128)(2,1)} %bitcast.10), channel_id=1, source_target_pairs={{0,8},{1,9},{2,10},{3,11},{4,12},{5,13},{6,14},{7,15},{8,0},{9,1},... | collective-permute-start | bytes 196616 | tf_op jit(solution)/shard_map/ppermute | solution.py:34
  5.9 7.8 %collective-permute-start.1 = (bf16[32,1024]{1,0:T(8,128)(2,1)}, bf16[32,1024]{1,0:T(8,128)(2,1)S(1)}, u32[]{:S(2)}, u32[]{:S(2)}) collective-permute-start(bf16[32,1024]{1,0:T(8,128)(2,1)} %bitcast.11), channel_id=1, source_target_pairs={{0,4},{1,5},{2,6},{3,7},{4,0},{5,1},{6,2},{7,3},{8,12},{9,13},{10,... | collective-permute-start | bytes 196616 | tf_op jit(solution)/shard_map/ppermute | solution.py:34
  9.0 9.5 %collective-permute-start.13 = (bf16[32,1024]{1,0:T(8,128)(2,1)S(1)}, bf16[32,1024]{1,0:T(8,128)(2,1)S(1)}, u32[]{:S(2)}, u32[]{:S(2)}) collective-permute-start(bf16[32,1024]{1,0:T(8,128)(2,1)S(1)} %collective-permute-done.7.refs_1_), channel_id=1, source_target_pairs={{0,2},{1,3},{2,0},{3,1},{4,6},{5,7},{6,4},{7,5},{8,10},{9,11},{10,... | collective-permute-start | bytes 196616 | tf_op jit(solution)/shard_map/ppermute | solution.py:34
  12.1 6.3 %collective-permute-start.12 = (bf16[32,1024]{1,0:T(8,128)(2,1)S(1)}, bf16[32,1024]{1,0:T(8,128)(2,1)S(1)}, u32[]{:S(2)}, u32[]{:S(2)}) collective-permute-start(bf16[32,1024]{1,0:T(8,128)(2,1)S(1)} %collective-permute-done.6.refs_0_), channel_id=1, source_target_pairs={{0,2},{1,3},{2,0},{3,1},{4,6},{5,7},{6,4},{7,5},{8,10},{9,11},{10,... | collective-permute-start | bytes 196616 | tf_op jit(solution)/shard_map/ppermute | solution.py:34
  13.6 4.8 %collective-permute-start.11 = (bf16[32,1024]{1,0:T(8,128)(2,1)S(1)}, bf16[32,1024]{1,0:T(8,128)(2,1)S(1)}, u32[]{:S(2)}, u32[]{:S(2)}) collective-permute-start(bf16[32,1024]{1,0:T(8,128)(2,1)S(1)} %collective-permute-done.1.refs_2_), channel_id=1, source_target_pairs={{0,2},{1,3},{2,0},{3,1},{4,6},{5,7},{6,4},{7,5},{8,10},{9,11},{10,... | collective-permute-start | bytes 196616 | tf_op jit(solution)/shard_map/ppermute | solution.py:34
  16.1 0.8 %copy-start.1 = (bf16[1024,32]{0,1:T(8,128)(2,1)S(1)}, bf16[1024,32]{0,1:T(8,128)(2,1)}, u32[]{:S(2)}) copy-start(bf16[1024,32]{0,1:T(8,128)(2,1)} %param.6) | copy-start | bytes 196612
  16.6 6.5 %collective-permute-start.10 = (f16[72,512]{1,0:T(8,128)(2,1)S(1)}, f16[72,512]{1,0:T(8,128)(2,1)S(1)}, u32[]{:S(2)}, u32[]{:S(2)}) collective-permute-start(f16[72,512]{1,0:T(8,128)(2,1)S(1)} %convert_element_type.48), channel_id=1, source_target_pairs={{0,17},{1,16},{2,19},{3,18},{4,21},{5,20},{6,23},{7,22},{8,25},{9,... | collective-permute-start | bytes 221192 | tf_op jit(solution)/shard_map/ppermute | solution.py:27
  16.9 5.6 %collective-permute-start = (bf16[32,1024]{1,0:T(8,128)(2,1)S(1)}, bf16[32,1024]{1,0:T(8,128)(2,1)S(1)}, u32[]{:S(2)}, u32[]{:S(2)}) collective-permute-start(bf16[32,1024]{1,0:T(8,128)(2,1)S(1)} %bitcast.13), channel_id=1, source_target_pairs={{0,2},{1,3},{2,0},{3,1},{4,6},{5,7},{6,4},{7,5},{8,10},{9,11},{10,... | collective-permute-start | bytes 196616 | tf_op jit(solution)/shard_map/ppermute | solution.py:34
  19.0 9.4 %collective-permute-start.16 = (f16[104,512]{1,0:T(8,128)(2,1)S(1)}, f16[104,512]{1,0:T(8,128)(2,1)S(1)}, u32[]{:S(2)}, u32[]{:S(2)}) collective-permute-start(f16[104,512]{1,0:T(8,128)(2,1)S(1)} %convert_element_type.52), channel_id=1, source_target_pairs={{0,17},{1,16},{2,19},{3,18},{4,21},{5,20},{6,23},{7,22},{8,25},{9,... | collective-permute-start | bytes 319496 | tf_op jit(solution)/shard_map/ppermute | solution.py:27
  20.3 9.6 %collective-permute-start.14 = (f16[104,512]{1,0:T(8,128)(2,1)S(1)}, f16[104,512]{1,0:T(8,128)(2,1)S(1)}, u32[]{:S(2)}, u32[]{:S(2)}) collective-permute-start(f16[104,512]{1,0:T(8,128)(2,1)S(1)} %convert_element_type.50), channel_id=1, source_target_pairs={{0,16},{1,17},{2,18},{3,19},{4,20},{5,21},{6,22},{7,23},{8,24},{9,... | collective-permute-start | bytes 319496 | tf_op jit(solution)/shard_map/ppermute | solution.py:27
  21.9 6.4 %collective-permute-start.8 = (f16[72,512]{1,0:T(8,128)(2,1)S(1)}, f16[72,512]{1,0:T(8,128)(2,1)S(1)}, u32[]{:S(2)}, u32[]{:S(2)}) collective-permute-start(f16[72,512]{1,0:T(8,128)(2,1)S(1)} %convert_element_type.46), channel_id=1, source_target_pairs={{0,16},{1,17},{2,18},{3,19},{4,20},{5,21},{6,22},{7,23},{8,24},{9,... | collective-permute-start | bytes 221192 | tf_op jit(solution)/shard_map/ppermute | solution.py:27
  23.0 13.0 %collective-permute-start.4 = (f32[96,512]{1,0:T(8,128)S(1)}, f32[96,512]{1,0:T(8,128)S(1)}, u32[]{:S(2)}, u32[]{:S(2)}) collective-permute-start(f32[96,512]{1,0:T(8,128)S(1)} %get-tuple-element.26), channel_id=1, source_target_pairs={{0,1},{1,0},{2,3},{3,2},{4,5},{5,4},{6,7},{7,6},{8,9},{9,8},{10,11... | collective-permute-start | bytes 589832 | tf_op jit(solution)/shard_map/ppermute | solution.py:34
  23.1 13.0 %collective-permute-start.15 = (f32[96,512]{1,0:T(8,128)S(1)}, f32[96,512]{1,0:T(8,128)S(1)}, u32[]{:S(2)}, u32[]{:S(2)}) collective-permute-start(f32[96,512]{1,0:T(8,128)S(1)} %get-tuple-element.34), channel_id=1, source_target_pairs={{0,1},{1,0},{2,3},{3,2},{4,5},{5,4},{6,7},{7,6},{8,9},{9,8},{10,11... | collective-permute-start | bytes 589832 | tf_op jit(solution)/shard_map/ppermute | solution.py:34
  28.4 7.7 %collective-permute-start.9 = (f32[64,512]{1,0:T(8,128)S(1)}, f32[64,512]{1,0:T(8,128)S(1)}, u32[]{:S(2)}, u32[]{:S(2)}) collective-permute-start(f32[64,512]{1,0:T(8,128)S(1)} %get-tuple-element.30), channel_id=1, source_target_pairs={{0,1},{1,0},{2,3},{3,2},{4,5},{5,4},{6,7},{7,6},{8,9},{9,8},{10,11... | collective-permute-start | bytes 393224 | tf_op jit(solution)/shard_map/ppermute | solution.py:34
  28.4 4.9 %collective-permute-start.5 = (f16[104,512]{1,0:T(8,128)(2,1)S(1)}, f16[104,512]{1,0:T(8,128)(2,1)S(1)}, u32[]{:S(2)}, u32[]{:S(2)}) collective-permute-start(f16[104,512]{1,0:T(8,128)(2,1)S(1)} %convert_element_type.44), channel_id=1, source_target_pairs={{0,17},{1,16},{2,19},{3,18},{4,21},{5,20},{6,23},{7,22},{8,25},{9,... | collective-permute-start | bytes 319496 | tf_op jit(solution)/shard_map/ppermute | solution.py:27
  29.9 6.1 %collective-permute-start.3 = (f16[104,512]{1,0:T(8,128)(2,1)S(1)}, f16[104,512]{1,0:T(8,128)(2,1)S(1)}, u32[]{:S(2)}, u32[]{:S(2)}) collective-permute-start(f16[104,512]{1,0:T(8,128)(2,1)S(1)} %convert_element_type.42), channel_id=1, source_target_pairs={{0,16},{1,17},{2,18},{3,19},{4,20},{5,21},{6,22},{7,23},{8,24},{9,... | collective-permute-start | bytes 319496 | tf_op jit(solution)/shard_map/ppermute | solution.py:27
  32.6 3.5 %copy-start = (s32[1,2]{1,0:T(1,128)S(1)}, s32[1,2]{1,0:T(1,128)}, u32[]{:S(2)}) copy-start(s32[1,2]{1,0:T(1,128)} %assign_ref.3) | copy-start | bytes 28
  44.1 13.2 %collective-permute-start.17 = (f16[520,512]{1,0:T(8,128)(2,1)S(1)}, f16[520,512]{1,0:T(8,128)(2,1)S(1)}, u32[]{:S(2)}, u32[]{:S(2)}) collective-permute-start(f16[520,512]{1,0:T(8,128)(2,1)S(1)} %convert_element_type.54), channel_id=1, source_target_pairs={{0,16},{16,0},{1,17},{17,1},{2,18},{18,2},{3,19},{19,3},{4,20},{20... | collective-permute-start | bytes 1597448 | tf_op jit(solution)/shard_map/ppermute | solution.py:34
where the time goes:
time: 59.6 us; the launch traced here: 59.4 us
  waiting for transfers between devices  22.1 us (37%)
  starting transfers between devices  18.5 us (31%)
  Pallas kernels  15.8 us (27%)
  local copies, waits for them, and re-layouts  1.81 us (3%)
  between operations  0.88 us (1%)
    ppermute x12, waiting for transfers between devices, moved(): lax.ppermute(block, axis, [(low, low ^ mask) for low in range(count) if l...  14 us
    pallas_call x8, Pallas kernels, call(): pl.pallas_call(body, out_shape=tuple((pltpu.VMEM(*shape) for shape in sha...  13.8 us
    ppermute x12, starting transfers between devices, moved(): lax.ppermute(block, axis, [(low, low ^ mask) for low in range(count) if l...  12.6 us
    ppermute x6, waiting for transfers between devices, crossed(): lax.ppermute(block, ('tok', 'blk'), [(low, low ^ half ^ mask) for low in...  8.07 us
    ppermute x6, starting transfers between devices, crossed(): lax.ppermute(block, ('tok', 'blk'), [(low, low ^ half ^ mask) for low in...  5.92 us
    pallas_call x1, Pallas kernels, stage(): pl.pallas_call(stage_body, out_shape=tuple((pltpu.VMEM(operand.shape, ope...  1.93 us
    unnamed x6, local copies, waits for them, and re-layouts  1.81 us
  transfers between devices with their start and end apart: 18, of which 6 were waited for; matrix products, arithmetic and copies ran while one was open for 2% of the time, Pallas kernels for 11%

commit v1 on v0

--- a/solution.py
+++ b/solution.py
@@ -195,8 +195,17 @@
     )(*operands)
 
 
-def squared_body(root_ref, out_ref):
+def mark_body(block_ref, out_ref):
+    out_ref[...] = block_ref[0:8, 0:128].astype(jnp.float32)
+
+
+def mark(block):
+    return call(mark_body, [((8, 128), jnp.float32)], [block])
+
+
+def fourth_body(assign_ref, root_ref, early_ref, late_ref, out_ref):
     value = split(root_ref[...])
+    value = split(multiply(value, value))
     out_ref[...] = multiply(value, value)
 
 
@@ -204,7 +213,7 @@
     assign_ref = refs[0]
     count = len(groups)
     stat_ref, warm_ref, fourth_ref = refs[1 + 2 * count : 4 + 2 * count]
-    root_ref, pay_ref, high_ref, low_ref, held_ref = refs[4 + 2 * count :]
+    root_ref, top_ref, bottom_ref, high_ref, low_ref, held_ref = refs[4 + 2 * count :]
     column, side = lax.axis_index("blk"), side_of(assign_ref)
     size = stat_ref.shape[-1]
     for group, masks in enumerate(groups):
@@ -228,22 +237,26 @@
     identity = jnp.where(eye_mask(size, size), 1.0, 0.0)
     factor = BETA * stat_ref[...] + (1.0 - BETA) * square + DAMPING * identity
     coupled = multiply(split(fourth_ref[...]), split(factor))
-    current = warm_ref[...]
-    for iteration in range(ITERS):
-        update = split((5.0 * identity - coupled) * 0.25)
-        current = multiply(split(current), update)
-        if iteration + 1 < ITERS:
-            update_square = split(multiply(update, update))
-            coupled = multiply(split(multiply(update_square, update_square)), split(coupled))
+    update = (5.0 * identity - coupled) * 0.25
+    parts = split(update)
+    update_square = multiply(parts, parts)
+    parts = split(update_square)
+    update_fourth = split(multiply(parts, parts))
+    inner = split(4.0 * update_square - 5.0 * update)
+    both_steps = (5.0 * update + multiply(update_fourth, inner)) * 0.25
+    current = multiply(split(warm_ref[...]), split(both_steps))
     root_ref[...] = current
     power = exponent_of(current)
     scaled = current * jnp.exp2(-power)
     diagonal = jnp.sum(scaled * identity, axis=0, keepdims=True)
     coarse = jnp.round(diagonal * 1024.0) * (1.0 / 1024.0)
-    pay_ref[0:size, :] = scaled * (1.0 - identity)
+    half = size // 2
+    scaled = scaled * (1.0 - identity)
+    top_ref[...] = scaled[:half, :]
+    bottom_ref[0:half, :] = scaled[half:, :]
     row = lax.broadcasted_iota(jnp.int32, (TAIL, size), 0)
     tail = jnp.where(row == 0, power, jnp.where(row == 1, coarse, diagonal - coarse))
-    pay_ref[size:, :] = tail
+    bottom_ref[half:, :] = tail
 
 
 def middle_body(assign_ref, root_ref, high_ref, low_ref, out_ref):
@@ -260,23 +273,42 @@
         out_ref[...] = multiply(oriented, split(root_ref[...]), ((0,), (0,)))
 
 
-def final_body(assign_ref, got_ref, middle_ref, out_ref):
-    size = middle_ref.shape[0]
-    half = size // 2
-    scale = jnp.exp2(got_ref[size : size + 1, :])
-    diagonal = got_ref[size + 1 : size + 2, :] + got_ref[size + 2 : size + 3, :]
-    other = jnp.where(eye_mask(size, size), diagonal, got_ref[0:size, :]) * scale
+def decoded(rows, tail, offset):
+    mask = lax.broadcasted_iota(jnp.int32, rows.shape, 0) + offset == lax.broadcasted_iota(
+        jnp.int32, rows.shape, 1
+    )
+    return jnp.where(mask, tail[1:2, :] + tail[2:3, :], rows) * jnp.exp2(tail[0:1, :])
+
+
+def bottom_body(assign_ref, got_ref, middle_ref, out_ref, tail_ref):
+    half = middle_ref.shape[0] // 2
+    tail = got_ref[half:, :]
+    tail_ref[...] = tail
+    other = split(decoded(got_ref[0:half, :], tail, half))
 
     @pl.when(side_of(assign_ref) == 0)
     def _():
-        out_ref[...] = multiply(split(middle_ref[0:half, :]), split(other))
+        out_ref[...] = multiply(split(middle_ref[0:half, half:]), other)
 
     @pl.when(side_of(assign_ref) != 0)
     def _():
-        out_ref[...] = multiply(split(other[half:, :]), split(middle_ref[...]))
-
-
-def call(body, shapes, operands, scratch=()):
+        out_ref[...] = multiply(other, split(middle_ref[...]))
+
+
+def top_body(assign_ref, got_ref, tail_ref, middle_ref, begun_ref, out_ref):
+    half = middle_ref.shape[0] // 2
+
+    @pl.when(side_of(assign_ref) == 0)
+    def _():
+        other = split(decoded(got_ref[...], tail_ref[...], 0))
+        out_ref[...] = begun_ref[...] + multiply(split(middle_ref[0:half, 0:half]), other)
+
+    @pl.when(side_of(assign_ref) != 0)
+    def _():
+        out_ref[...] = begun_ref[...]
+
+
+def call(body, shapes, operands, scratch=(), kept=True):
     smem = pl.BlockSpec(memory_space=pltpu.SMEM)
     vmem = pl.BlockSpec(memory_space=pltpu.VMEM)
     whole = [operand.dtype == jnp.int32 for operand in operands]
@@ -286,7 +318,7 @@
     ]
     return pl.pallas_call(
         body,
-        out_shape=tuple(pltpu.VMEM(*shape) for shape in shapes),
+        out_shape=tuple((pltpu.VMEM if kept else jax.ShapeDtypeStruct)(*shape) for shape in shapes),
         in_specs=[smem if scalar else vmem for scalar in whole],
         out_specs=tuple(vmem for _ in shapes),
         scratch_shapes=list(scratch),
@@ -309,11 +341,11 @@
     for mask in far:
         parts[mask | 2] = moved(parts[mask], "blk", 2)
     grads = [grad, moved(grad_out, "blk", 1)]
-    (second,) = call(squared_body, [(square, jnp.float32)], [warm])
-    (fourth,) = call(squared_body, [(square, jnp.float32)], [second])
+    marks = mark(parts[0]) + mark(grads[0])
+    (fourth,) = call(fourth_body, [(square, jnp.float32)], [assign, warm, *marks])
     groups = []
     operands = [assign]
-    for masks in ([0, 2] + far[:1], far[1:], [mask | 2 for mask in far]):
+    for masks in ([0, 2] + far[:1], far[1:] + [far[0] | 2], [mask | 2 for mask in far[1:]]):
         own, own_pay, beside, beside_pay = partial_chunk(
             [parts[mask] for mask in masks], grads, scaling
         )
@@ -322,20 +354,33 @@
         beside = moved(beside, "blk", 1)
         operands += [own, got.astype(jnp.float32), beside, got_beside.astype(jnp.float32)]
         groups += [masks, [mask | 1 for mask in masks]]
-    own_root, pay, high, low = call(
+    half = size // 2
+    own_root, top, bottom, high, low = call(
         functools.partial(root_body, groups=groups, all_tokens=all_tokens),
         [
             (square, jnp.float32),
-            ((size + TAIL, size), jnp.float32),
+            ((half, size), jnp.float32),
+            ((half + TAIL, size), jnp.float32),
             (square, jnp.bfloat16),
             (square, jnp.bfloat16),
         ],
         operands + [stat, warm, fourth],
         [pltpu.VMEM(square, jnp.float32)],
     )
-    got = moved(pay.astype(jnp.float16), "tok", 1).astype(jnp.float32)
+    bottom = crossed(bottom.astype(jnp.float16), 0)
+    top = crossed(top.astype(jnp.float16), 0)
     (middle,) = call(middle_body, [(square, jnp.float32)], [assign, own_root, high, low])
-    (precond,) = call(final_body, [((size // 2, size), jnp.float32)], [assign, got, middle])
+    begun, tail = call(
+        bottom_body,
+        [((half, size), jnp.float32), ((TAIL, size), jnp.float32)],
+        [assign, bottom.astype(jnp.float32), middle],
+    )
+    (precond,) = call(
+        top_body,
+        [((half, size), jnp.float32)],
+        [assign, top.astype(jnp.float32), tail, middle, begun],
+        kept=False,
+    )
     return (own_root[None, None], precond[None, None])
 
 

time: 59.6 us -> 60.2 us (1.010)
  Pallas kernels: 15.8 us -> 16.9 us
  waiting for transfers between devices: 22.1 us -> 21.2 us
    ppermute x12 -> x11, waiting for transfers between devices: 14 us -> 5.39 us  [moved(): lax.ppermute(block, axis, [(low, low ^ mask) for low in range(count) if l...]
    ppermute x6 -> x8, waiting for transfers between devices: 8.07 us -> 15.8 us  [crossed(): lax.ppermute(block, ('tok', 'blk'), [(low, low ^ half ^ mask) for low in...]
    ppermute x12 -> x11, starting transfers between devices: 12.6 us -> 11 us  [moved(): lax.ppermute(block, axis, [(low, low ^ mask) for low in range(count) if l...]
    ppermute x6 -> x8, starting transfers between devices: 5.92 us -> 7.38 us  [crossed(): lax.ppermute(block, ('tok', 'blk'), [(low, low ^ half ^ mask) for low in...]
    pallas_call x8 -> x10, Pallas kernels: 13.8 us -> 14.9 us  [call(): pl.pallas_call(body, out_shape=tuple(((pltpu.VMEM if kept else jax.ShapeD...]
    unnamed x6 -> x5, local copies, waits for them, and re-layouts: 1.81 us -> 2.36 us
  transfers between devices with their start and end apart: 18 -> 19, of which waited for: 6 -> 7; matrix products, arithmetic and copies ran while one was open for 2% -> 2% of each run, Pallas kernels for 11% -> 12%
where the time goes in v1:
time: 60.2 us; the launch traced here: 60 us
  waiting for transfers between devices  21.2 us (35%)
  starting transfers between devices  18.3 us (30%)
  Pallas kernels  16.9 us (28%)
  local copies, waits for them, and re-layouts  2.36 us (4%)
  between operations  0.89 us (1%)
    ppermute x8, waiting for transfers between devices, crossed(): lax.ppermute(block, ('tok', 'blk'), [(low, low ^ half ^ mask) for low in...  15.8 us
    pallas_call x10, Pallas kernels, call(): pl.pallas_call(body, out_shape=tuple(((pltpu.VMEM if kept else jax.ShapeD...  14.9 us
    ppermute x11, starting transfers between devices, moved(): lax.ppermute(block, axis, [(low, low ^ mask) for low in range(count) if l...  11 us
    ppermute x8, starting transfers between devices, crossed(): lax.ppermute(block, ('tok', 'blk'), [(low, low ^ half ^ mask) for low in...  7.38 us
    ppermute x11, waiting for transfers between devices, moved(): lax.ppermute(block, axis, [(low, low ^ mask) for low in range(count) if l...  5.39 us
    unnamed x5, local copies, waits for them, and re-layouts  2.36 us
    pallas_call x1, Pallas kernels, stage(): pl.pallas_call(stage_body, out_shape=tuple((pltpu.VMEM(operand.shape, ope...  1.93 us
  transfers between devices with their start and end apart: 19, of which 7 were waited for; matrix products, arithmetic and copies ran while one was open for 2% of the time, Pallas kernels for 12%

profile of v1, /device:TPU:0, one launch (start us, length us, event | category | flops | bytes accessed | tf_op | source)
XLA Modules:
  0.0 60.0 jit_solution(6159270377061098571)
XLA Ops:
  0.6 0.6 collective-permute-start.2
  1.2 4.7 %collective-permute-start.7 = (bf16[32,1024]{1,0:T(8,128)(2,1)}, bf16[32,1024]{1,0:T(8,128)(2,1)S(1)}, u32[]{:S(2)}, u32[]{:S(2)}) collective-permute-start(bf16[32,1024]{1,0:T(8,128)(2,1)} %bitcast.9), channel_id=1, source_target_pairs={{0,12},{1,13},{2,14},{3,15},{4,8},{5,9},{6,10},{7,11},{8,4},{9,5},... | collective-permute-start | bytes 196616 | tf_op jit(solution)/shard_map/ppermute | solution.py:34
  5.9 0.0 collective-permute-start.6
  5.9 0.6 %collective-permute-start.1 = (bf16[32,1024]{1,0:T(8,128)(2,1)}, bf16[32,1024]{1,0:T(8,128)(2,1)S(1)}, u32[]{:S(2)}, u32[]{:S(2)}) collective-permute-start(bf16[32,1024]{1,0:T(8,128)(2,1)} %bitcast.11), channel_id=1, source_target_pairs={{0,4},{1,5},{2,6},{3,7},{4,0},{5,1},{6,2},{7,3},{8,12},{9,13},{10,... | collective-permute-start | bytes 196616 | tf_op jit(solution)/shard_map/ppermute | solution.py:34
  6.5 2.5 %collective-permute-done.7.refs_1_ = bf16[32,1024]{1,0:T(8,128)(2,1)S(1)} collective-permute-done((bf16[32,1024]{1,0:T(8,128)(2,1)}, bf16[32,1024]{1,0:T(8,128)(2,1)S(1)}, u32[]{:S(2)}, u32[]{:S(2)}) %collective-permute-start.7) | collective-permute-done | bytes 65568 | tf_op jit(solution)/shard_map/ppermute | solution.py:34
  9.0 1.5 %collective-permute-start.13 = (bf16[32,1024]{1,0:T(8,128)(2,1)S(1)}, bf16[32,1024]{1,0:T(8,128)(2,1)S(1)}, u32[]{:S(2)}, u32[]{:S(2)}) collective-permute-start(bf16[32,1024]{1,0:T(8,128)(2,1)S(1)} %collective-permute-done.7.refs_1_), channel_id=1, source_target_pairs={{0,2},{1,3},{2,0},{3,1},{4,6},{5,7},{6,4},{7,5},{8,10},{9,11},{10,... | collective-permute-start | bytes 196616 | tf_op jit(solution)/shard_map/ppermute | solution.py:34
  10.5 1.6 %collective-permute-done.6.refs_0_ = bf16[32,1024]{1,0:T(8,128)(2,1)S(1)} collective-permute-done((bf16[32,1024]{1,0:T(8,128)(2,1)}, bf16[32,1024]{1,0:T(8,128)(2,1)S(1)}, u32[]{:S(2)}, u32[]{:S(2)}) %collective-permute-start.6) | collective-permute-done | bytes 65568 | tf_op jit(solution)/shard_map/ppermute | solution.py:34
  12.1 1.5 %collective-permute-start.12 = (bf16[32,1024]{1,0:T(8,128)(2,1)S(1)}, bf16[32,1024]{1,0:T(8,128)(2,1)S(1)}, u32[]{:S(2)}, u32[]{:S(2)}) collective-permute-start(bf16[32,1024]{1,0:T(8,128)(2,1)S(1)} %collective-permute-done.6.refs_0_), channel_id=1, source_target_pairs={{0,2},{1,3},{2,0},{3,1},{4,6},{5,7},{6,4},{7,5},{8,10},{9,11},{10,... | collective-permute-start | bytes 196616 | tf_op jit(solution)/shard_map/ppermute | solution.py:34
  13.6 0.0 collective-permute-done.1.refs_2_
  13.6 0.5 collective-permute-start.8
  14.1 1.9 %stage.1 = (bf16[32,1024]{1,0:T(8,128)(2,1)S(1)}, bf16[1024,512]{1,0:T(8,128)(2,1)S(1)}, f32[512,512]{1,0:T(8,128)S(1)}, f32[512,512]{1,0:T(8,128)S(1)}) custom-call(bf16[32,1024]{1,0:T(8,128)(2,1)} %bitcast.12, bf16[1024,512]{1,0:T(8,128)(2,1)} %refs_1_.1, f32[512,512]{1,0:T(8,128)} %bitcast.6, f32[512,512]{1,0:T(8,128)} %bitcast.7), custom_call_target="tpu_custom_call" | custom-call | tf_op jit(solution)/shard_map/stage/pallas_call | solution.py:187
  16.1 0.9 %collective-permute-done.12.refs_0_ = bf16[32,1024]{1,0:T(8,128)(2,1)S(1)} collective-permute-done((bf16[32,1024]{1,0:T(8,128)(2,1)S(1)}, bf16[32,1024]{1,0:T(8,128)(2,1)S(1)}, u32[]{:S(2)}, u32[]{:S(2)}) %collective-permute-start.12) | collective-permute-done | bytes 65568 | tf_op jit(solution)/shard_map/ppermute | solution.py:34
  17.0 0.0 collective-permute-done.2.refs_4_.refs_3_
  17.0 0.5 shard_map.70
  17.5 0.0 copy-start.1
  17.6 0.1 collective-permute-start.16
  17.6 0.7 %copy-done.1 = bf16[1024,32]{0,1:T(8,128)(2,1)S(1)} copy-done((bf16[1024,32]{0,1:T(8,128)(2,1)S(1)}, bf16[1024,32]{0,1:T(8,128)(2,1)}, u32[]{:S(2)}) %copy-start.1) | copy-done | bytes 65560
  18.4 1.0 %collective-permute-start = (bf16[32,1024]{1,0:T(8,128)(2,1)S(1)}, bf16[32,1024]{1,0:T(8,128)(2,1)S(1)}, u32[]{:S(2)}, u32[]{:S(2)}) collective-permute-start(bf16[32,1024]{1,0:T(8,128)(2,1)S(1)} %bitcast.13), channel_id=1, source_target_pairs={{0,2},{1,3},{2,0},{3,1},{4,6},{5,7},{6,4},{7,5},{8,10},{9,11},{10,... | collective-permute-start | bytes 196616 | tf_op jit(solution)/shard_map/ppermute | solution.py:34
  19.4 0.0 collective-permute-done.8.refs_2_
  19.4 0.5 shard_map.69
  19.9 0.8 %collective-permute-start.11 = (f16[104,512]{1,0:T(8,128)(2,1)S(1)}, f16[104,512]{1,0:T(8,128)(2,1)S(1)}, u32[]{:S(2)}, u32[]{:S(2)}) collective-permute-start(f16[104,512]{1,0:T(8,128)(2,1)S(1)} %convert_element_type.54), channel_id=1, source_target_pairs={{0,17},{1,16},{2,19},{3,18},{4,21},{5,20},{6,23},{7,22},{8,25},{9,... | collective-permute-start | bytes 319496 | tf_op jit(solution)/shard_map/ppermute | solution.py:27
  20.7 1.6 %collective-permute-start.9 = (f16[104,512]{1,0:T(8,128)(2,1)S(1)}, f16[104,512]{1,0:T(8,128)(2,1)S(1)}, u32[]{:S(2)}, u32[]{:S(2)}) collective-permute-start(f16[104,512]{1,0:T(8,128)(2,1)S(1)} %convert_element_type.52), channel_id=1, source_target_pairs={{0,16},{1,17},{2,18},{3,19},{4,20},{5,21},{6,22},{7,23},{8,24},{9,... | collective-permute-start | bytes 319496 | tf_op jit(solution)/shard_map/ppermute | solution.py:27
  22.3 0.6 %collective-permute-start.14 = (f16[72,512]{1,0:T(8,128)(2,1)S(1)}, f16[72,512]{1,0:T(8,128)(2,1)S(1)}, u32[]{:S(2)}, u32[]{:S(2)}) collective-permute-start(f16[72,512]{1,0:T(8,128)(2,1)S(1)} %convert_element_type.56), channel_id=1, source_target_pairs={{0,16},{1,17},{2,18},{3,19},{4,20},{5,21},{6,22},{7,23},{8,24},{9,... | collective-permute-start | bytes 221192 | tf_op jit(solution)/shard_map/ppermute | solution.py:27
  22.9 0.4 collective-permute-done.refs_1_
  23.2 0.5 shard_map.68
  23.8 0.1 collective-permute-start.4
  23.8 0.0 collective-permute-done.16
  23.8 0.5 collective-permute-start.10
  24.3 4.8 %collective-permute-done.14 = f16[72,512]{1,0:T(8,128)(2,1)S(1)} collective-permute-done((f16[72,512]{1,0:T(8,128)(2,1)S(1)}, f16[72,512]{1,0:T(8,128)(2,1)S(1)}, u32[]{:S(2)}, u32[]{:S(2)}) %collective-permute-start.14) | collective-permute-done | bytes 73760 | tf_op jit(solution)/shard_map/ppermute | solution.py:27
  29.1 0.0 collective-permute-start.15
  29.1 0.0 collective-permute-done.11
  29.2 1.3 %collective-permute-start.5 = (f16[104,512]{1,0:T(8,128)(2,1)S(1)}, f16[104,512]{1,0:T(8,128)(2,1)S(1)}, u32[]{:S(2)}, u32[]{:S(2)}) collective-permute-start(f16[104,512]{1,0:T(8,128)(2,1)S(1)} %convert_element_type.50), channel_id=1, source_target_pairs={{0,17},{1,16},{2,19},{3,18},{4,21},{5,20},{6,23},{7,22},{8,25},{9,... | collective-permute-start | bytes 319496 | tf_op jit(solution)/shard_map/ppermute | solution.py:27
  30.4 0.0 collective-permute-done.9
  30.4 0.9 %collective-permute-start.3 = (f16[104,512]{1,0:T(8,128)(2,1)S(1)}, f16[104,512]{1,0:T(8,128)(2,1)S(1)}, u32[]{:S(2)}, u32[]{:S(2)}) collective-permute-start(f16[104,512]{1,0:T(8,128)(2,1)S(1)} %convert_element_type.48), channel_id=1, source_target_pairs={{0,16},{1,17},{2,18},{3,19},{4,20},{5,21},{6,22},{7,23},{8,24},{9,... | collective-permute-start | bytes 319496 | tf_op jit(solution)/shard_map/ppermute | solution.py:27
  31.4 0.7 %copy-done = s32[1,2]{1,0:T(1,128)S(1)} copy-done((s32[1,2]{1,0:T(1,128)S(1)}, s32[1,2]{1,0:T(1,128)}, u32[]{:S(2)}) %copy-start) | copy-done | bytes 32
  32.0 2.4 %shard_map.73.refs_15_ = f32[512,512]{1,0:T(8,128)S(1)} custom-call(s32[1,2]{1,0:T(1,128)S(1)} %copy-done, f32[512,512]{1,0:T(8,128)S(1)} %get-tuple-element.40.root_ref.refs_14_, f32[8,128]{1,0:T(8,128)S(1)} %shard_map.71.early_ref, f32[8,128]{1,0:T(8,128)S(1)} %shard_map.72.late_ref), custom_call_target="tpu_custom_call" | custom-call | tf_op jit(solution)/shard_map/pallas_call | solution.py:319
  34.6 2.2 %collective-permute-done.3 = f16[104,512]{1,0:T(8,128)(2,1)S(1)} collective-permute-done((f16[104,512]{1,0:T(8,128)(2,1)S(1)}, f16[104,512]{1,0:T(8,128)(2,1)S(1)}, u32[]{:S(2)}, u32[]{:S(2)}) %collective-permute-start.3) | collective-permute-done | bytes 106528 | tf_op jit(solution)/shard_map/ppermute | solution.py:27
  36.8 0.0 collective-permute-done.4.refs_3_
  36.8 7.0 %shard_map.74 = (f32[512,512]{1,0:T(8,128)S(1)}, f32[256,512]{1,0:T(8,128)S(1)}, f32[264,512]{1,0:T(8,128)S(1)}, bf16[512,512]{1,0:T(8,128)(2,1)S(1)}, bf16[512,512]{1,0:T(8,128)(2,1)S(1)}) custom-call(s32[1,2]{1,0:T(1,128)S(1)} %copy-done, f32[96,512]{1,0:T(8,128)S(1)} %get-tuple-element.27.refs_1_, f32[104,512]{1,0:T(8,128)S(1)} %convert_element_type.49.refs_2_, ...), custom_call_target="tpu_custom_call" | custom-call | tf_op jit(solution)/shard_map/pallas_call | solution.py:319
  43.9 0.9 %collective-permute-start.18 = (f16[264,512]{1,0:T(8,128)(2,1)S(1)}, f16[264,512]{1,0:T(8,128)(2,1)S(1)}, u32[]{:S(2)}, u32[]{:S(2)}) collective-permute-start(f16[264,512]{1,0:T(8,128)(2,1)S(1)} %convert_element_type.62), channel_id=1, source_target_pairs={{0,16},{1,17},{2,18},{3,19},{4,20},{5,21},{6,22},{7,23},{8,24},{9,... | collective-permute-start | bytes 811016 | tf_op jit(solution)/shard_map/ppermute | solution.py:27
  44.9 1.2 %collective-permute-start.17 = (f16[256,512]{1,0:T(8,128)(2,1)S(1)}, f16[256,512]{1,0:T(8,128)(2,1)S(1)}, u32[]{:S(2)}, u32[]{:S(2)}) collective-permute-start(f16[256,512]{1,0:T(8,128)(2,1)S(1)} %convert_element_type.60), channel_id=1, source_target_pairs={{0,16},{1,17},{2,18},{3,19},{4,20},{5,21},{6,22},{7,23},{8,24},{9,... | collective-permute-start | bytes 786440 | tf_op jit(solution)/shard_map/ppermute | solution.py:27
  46.1 1.0 %copy.7 = f32[1,1,512,512]{3,2,1,0:T(8,128)} copy(f32[1,1,512,512]{3,2,1,0:T(8,128)S(1)} %bitcast.5) | data formatting | bytes 2097152
  47.1 1.2 %shard_map.75.middle_ref = f32[512,512]{1,0:T(8,128)S(1)} custom-call(s32[1,2]{1,0:T(1,128)S(1)} %copy-done, f32[512,512]{1,0:T(8,128)S(1)} %get-tuple-element.41.root_ref, bf16[512,512]{1,0:T(8,128)(2,1)S(1)} %get-tuple-element.44.high_ref, bf16[512,512]{1,0:T(8,128)(2,1)S(1)} %get-tuple-element.45.low_ref), custom_call_target="tpu_custom_call" | custom-call | tf_op jit(solution)/shard_map/pallas_call | solution.py:319
  48.3 8.8 %collective-permute-done.17 = f16[256,512]{1,0:T(8,128)(2,1)S(1)} collective-permute-done((f16[256,512]{1,0:T(8,128)(2,1)S(1)}, f16[256,512]{1,0:T(8,128)(2,1)S(1)}, u32[]{:S(2)}, u32[]{:S(2)}) %collective-permute-start.17) | collective-permute-done | bytes 262176 | tf_op jit(solution)/shard_map/ppermute | solution.py:27
  57.0 0.1 convert_element_type.61.got_ref
  57.1 0.1 convert_element_type.63.got_ref
  57.2 1.0 %shard_map.76 = (f32[256,512]{1,0:T(8,128)S(1)}, f32[8,512]{1,0:T(8,128)S(1)}) custom-call(s32[1,2]{1,0:T(1,128)S(1)} %copy-done, f32[264,512]{1,0:T(8,128)S(1)} %convert_element_type.63.got_ref, f32[512,512]{1,0:T(8,128)S(1)} %shard_map.75.middle_ref), custom_call_target="tpu_custom_call" | custom-call | tf_op jit(solution)/shard_map/pallas_call | solution.py:319
  58.2 1.8 %shard_map.77 = f32[256,512]{1,0:T(8,128)} custom-call(s32[1,2]{1,0:T(1,128)S(1)} %copy-done, f32[256,512]{1,0:T(8,128)S(1)} %convert_element_type.61.got_ref, f32[8,512]{1,0:T(8,128)S(1)} %get-tuple-element.46.tail_ref, f32[512,512]{1,0:T(8,128)S(1)} %shard_map.75.middle_ref, f32[256,512]{1,0:T(8,128)S(1)} %get-tuple-element.47.begun_ref), custom_call_target="tpu_custom_call" | custom-call | tf_op jit(solution)/shard_map/pallas_call | solution.py:319
  (22 shorter events, 0.3 us)
Async XLA Ops:
  0.6 16.4 %collective-permute-start.2 = (bf16[1024,512]{1,0:T(8,128)(2,1)}, bf16[1024,512]{1,0:T(8,128)(2,1)S(1)}, u32[]{:S(2)}, u32[]{:S(2)}) collective-permute-start(bf16[1024,512]{1,0:T(8,128)(2,1)} %refs_1_.1), channel_id=1, source_target_pairs={{0,1},{1,0},{2,3},{3,2},{4,5},{5,4},{6,7},{7,6},{8,9},{9,8},{10,11... | collective-permute-start | bytes 3145736 | tf_op jit(solution)/shard_map/ppermute | solution.py:34
  1.2 7.8 %collective-permute-start.7 = (bf16[32,1024]{1,0:T(8,128)(2,1)}, bf16[32,1024]{1,0:T(8,128)(2,1)S(1)}, u32[]{:S(2)}, u32[]{:S(2)}) collective-permute-start(bf16[32,1024]{1,0:T(8,128)(2,1)} %bitcast.9), channel_id=1, source_target_pairs={{0,12},{1,13},{2,14},{3,15},{4,8},{5,9},{6,10},{7,11},{8,4},{9,5},... | collective-permute-start | bytes 196616 | tf_op jit(solution)/shard_map/ppermute | solution.py:34
  5.9 6.3 %collective-permute-start.6 = (bf16[32,1024]{1,0:T(8,128)(2,1)}, bf16[32,1024]{1,0:T(8,128)(2,1)S(1)}, u32[]{:S(2)}, u32[]{:S(2)}) collective-permute-start(bf16[32,1024]{1,0:T(8,128)(2,1)} %bitcast.10), channel_id=1, source_target_pairs={{0,8},{1,9},{2,10},{3,11},{4,12},{5,13},{6,14},{7,15},{8,0},{9,1},... | collective-permute-start | bytes 196616 | tf_op jit(solution)/shard_map/ppermute | solution.py:34
  5.9 7.8 %collective-permute-start.1 = (bf16[32,1024]{1,0:T(8,128)(2,1)}, bf16[32,1024]{1,0:T(8,128)(2,1)S(1)}, u32[]{:S(2)}, u32[]{:S(2)}) collective-permute-start(bf16[32,1024]{1,0:T(8,128)(2,1)} %bitcast.11), channel_id=1, source_target_pairs={{0,4},{1,5},{2,6},{3,7},{4,0},{5,1},{6,2},{7,3},{8,12},{9,13},{10,... | collective-permute-start | bytes 196616 | tf_op jit(solution)/shard_map/ppermute | solution.py:34
  9.0 7.1 %collective-permute-start.13 = (bf16[32,1024]{1,0:T(8,128)(2,1)S(1)}, bf16[32,1024]{1,0:T(8,128)(2,1)S(1)}, u32[]{:S(2)}, u32[]{:S(2)}) collective-permute-start(bf16[32,1024]{1,0:T(8,128)(2,1)S(1)} %collective-permute-done.7.refs_1_), channel_id=1, source_target_pairs={{0,2},{1,3},{2,0},{3,1},{4,6},{5,7},{6,4},{7,5},{8,10},{9,11},{10,... | collective-permute-start | bytes 196616 | tf_op jit(solution)/shard_map/ppermute | solution.py:34
  12.1 4.9 %collective-permute-start.12 = (bf16[32,1024]{1,0:T(8,128)(2,1)S(1)}, bf16[32,1024]{1,0:T(8,128)(2,1)S(1)}, u32[]{:S(2)}, u32[]{:S(2)}) collective-permute-start(bf16[32,1024]{1,0:T(8,128)(2,1)S(1)} %collective-permute-done.6.refs_0_), channel_id=1, source_target_pairs={{0,2},{1,3},{2,0},{3,1},{4,6},{5,7},{6,4},{7,5},{8,10},{9,11},{10,... | collective-permute-start | bytes 196616 | tf_op jit(solution)/shard_map/ppermute | solution.py:34
  13.6 5.7 %collective-permute-start.8 = (bf16[32,1024]{1,0:T(8,128)(2,1)S(1)}, bf16[32,1024]{1,0:T(8,128)(2,1)S(1)}, u32[]{:S(2)}, u32[]{:S(2)}) collective-permute-start(bf16[32,1024]{1,0:T(8,128)(2,1)S(1)} %collective-permute-done.1.refs_2_), channel_id=1, source_target_pairs={{0,2},{1,3},{2,0},{3,1},{4,6},{5,7},{6,4},{7,5},{8,10},{9,11},{10,... | collective-permute-start | bytes 196616 | tf_op jit(solution)/shard_map/ppermute | solution.py:34
  17.5 0.8 %copy-start.1 = (bf16[1024,32]{0,1:T(8,128)(2,1)S(1)}, bf16[1024,32]{0,1:T(8,128)(2,1)}, u32[]{:S(2)}) copy-start(bf16[1024,32]{0,1:T(8,128)(2,1)} %param.6) | copy-start | bytes 196612
  17.6 6.3 %collective-permute-start.16 = (f16[72,512]{1,0:T(8,128)(2,1)S(1)}, f16[72,512]{1,0:T(8,128)(2,1)S(1)}, u32[]{:S(2)}, u32[]{:S(2)}) collective-permute-start(f16[72,512]{1,0:T(8,128)(2,1)S(1)} %convert_element_type.58), channel_id=1, source_target_pairs={{0,17},{1,16},{2,19},{3,18},{4,21},{5,20},{6,23},{7,22},{8,25},{9,... | collective-permute-start | bytes 221192 | tf_op jit(solution)/shard_map/ppermute | solution.py:27
  18.4 4.9 %collective-permute-start = (bf16[32,1024]{1,0:T(8,128)(2,1)S(1)}, bf16[32,1024]{1,0:T(8,128)(2,1)S(1)}, u32[]{:S(2)}, u32[]{:S(2)}) collective-permute-start(bf16[32,1024]{1,0:T(8,128)(2,1)S(1)} %bitcast.13), channel_id=1, source_target_pairs={{0,2},{1,3},{2,0},{3,1},{4,6},{5,7},{6,4},{7,5},{8,10},{9,11},{10,... | collective-permute-start | bytes 196616 | tf_op jit(solution)/shard_map/ppermute | solution.py:34
  19.9 9.2 %collective-permute-start.11 = (f16[104,512]{1,0:T(8,128)(2,1)S(1)}, f16[104,512]{1,0:T(8,128)(2,1)S(1)}, u32[]{:S(2)}, u32[]{:S(2)}) collective-permute-start(f16[104,512]{1,0:T(8,128)(2,1)S(1)} %convert_element_type.54), channel_id=1, source_target_pairs={{0,17},{1,16},{2,19},{3,18},{4,21},{5,20},{6,23},{7,22},{8,25},{9,... | collective-permute-start | bytes 319496 | tf_op jit(solution)/shard_map/ppermute | solution.py:27
  20.7 9.7 %collective-permute-start.9 = (f16[104,512]{1,0:T(8,128)(2,1)S(1)}, f16[104,512]{1,0:T(8,128)(2,1)S(1)}, u32[]{:S(2)}, u32[]{:S(2)}) collective-permute-start(f16[104,512]{1,0:T(8,128)(2,1)S(1)} %convert_element_type.52), channel_id=1, source_target_pairs={{0,16},{1,17},{2,18},{3,19},{4,20},{5,21},{6,22},{7,23},{8,24},{9,... | collective-permute-start | bytes 319496 | tf_op jit(solution)/shard_map/ppermute | solution.py:27
  22.3 6.8 %collective-permute-start.14 = (f16[72,512]{1,0:T(8,128)(2,1)S(1)}, f16[72,512]{1,0:T(8,128)(2,1)S(1)}, u32[]{:S(2)}, u32[]{:S(2)}) collective-permute-start(f16[72,512]{1,0:T(8,128)(2,1)S(1)} %convert_element_type.56), channel_id=1, source_target_pairs={{0,16},{1,17},{2,18},{3,19},{4,20},{5,21},{6,22},{7,23},{8,24},{9,... | collective-permute-start | bytes 221192 | tf_op jit(solution)/shard_map/ppermute | solution.py:27
  23.8 13.1 %collective-permute-start.4 = (f32[96,512]{1,0:T(8,128)S(1)}, f32[96,512]{1,0:T(8,128)S(1)}, u32[]{:S(2)}, u32[]{:S(2)}) collective-permute-start(f32[96,512]{1,0:T(8,128)S(1)} %get-tuple-element.29), channel_id=1, source_target_pairs={{0,1},{1,0},{2,3},{3,2},{4,5},{5,4},{6,7},{7,6},{8,9},{9,8},{10,11... | collective-permute-start | bytes 589832 | tf_op jit(solution)/shard_map/ppermute | solution.py:34
  23.8 13.0 %collective-permute-start.10 = (f32[96,512]{1,0:T(8,128)S(1)}, f32[96,512]{1,0:T(8,128)S(1)}, u32[]{:S(2)}, u32[]{:S(2)}) collective-permute-start(f32[96,512]{1,0:T(8,128)S(1)} %get-tuple-element.33), channel_id=1, source_target_pairs={{0,1},{1,0},{2,3},{3,2},{4,5},{5,4},{6,7},{7,6},{8,9},{9,8},{10,11... | collective-permute-start | bytes 589832 | tf_op jit(solution)/shard_map/ppermute | solution.py:34
  29.1 7.7 %collective-permute-start.15 = (f32[64,512]{1,0:T(8,128)S(1)}, f32[64,512]{1,0:T(8,128)S(1)}, u32[]{:S(2)}, u32[]{:S(2)}) collective-permute-start(f32[64,512]{1,0:T(8,128)S(1)} %get-tuple-element.37), channel_id=1, source_target_pairs={{0,1},{1,0},{2,3},{3,2},{4,5},{5,4},{6,7},{7,6},{8,9},{9,8},{10,11... | collective-permute-start | bytes 393224 | tf_op jit(solution)/shard_map/ppermute | solution.py:34
  29.2 5.4 %collective-permute-start.5 = (f16[104,512]{1,0:T(8,128)(2,1)S(1)}, f16[104,512]{1,0:T(8,128)(2,1)S(1)}, u32[]{:S(2)}, u32[]{:S(2)}) collective-permute-start(f16[104,512]{1,0:T(8,128)(2,1)S(1)} %convert_element_type.50), channel_id=1, source_target_pairs={{0,17},{1,16},{2,19},{3,18},{4,21},{5,20},{6,23},{7,22},{8,25},{9,... | collective-permute-start | bytes 319496 | tf_op jit(solution)/shard_map/ppermute | solution.py:27
  30.4 6.3 %collective-permute-start.3 = (f16[104,512]{1,0:T(8,128)(2,1)S(1)}, f16[104,512]{1,0:T(8,128)(2,1)S(1)}, u32[]{:S(2)}, u32[]{:S(2)}) collective-permute-start(f16[104,512]{1,0:T(8,128)(2,1)S(1)} %convert_element_type.48), channel_id=1, source_target_pairs={{0,16},{1,17},{2,18},{3,19},{4,20},{5,21},{6,22},{7,23},{8,24},{9,... | collective-permute-start | bytes 319496 | tf_op jit(solution)/shard_map/ppermute | solution.py:27
  31.4 0.7 %copy-start = (s32[1,2]{1,0:T(1,128)S(1)}, s32[1,2]{1,0:T(1,128)}, u32[]{:S(2)}) copy-start(s32[1,2]{1,0:T(1,128)} %assign_ref.7) | copy-start | bytes 28
  43.9 13.2 %collective-permute-start.18 = (f16[264,512]{1,0:T(8,128)(2,1)S(1)}, f16[264,512]{1,0:T(8,128)(2,1)S(1)}, u32[]{:S(2)}, u32[]{:S(2)}) collective-permute-start(f16[264,512]{1,0:T(8,128)(2,1)S(1)} %convert_element_type.62), channel_id=1, source_target_pairs={{0,16},{1,17},{2,18},{3,19},{4,20},{5,21},{6,22},{7,23},{8,24},{9,... | collective-permute-start | bytes 811016 | tf_op jit(solution)/shard_map/ppermute | solution.py:27
  44.9 12.2 %collective-permute-start.17 = (f16[256,512]{1,0:T(8,128)(2,1)S(1)}, f16[256,512]{1,0:T(8,128)(2,1)S(1)}, u32[]{:S(2)}, u32[]{:S(2)}) collective-permute-start(f16[256,512]{1,0:T(8,128)(2,1)S(1)} %convert_element_type.60), channel_id=1, source_target_pairs={{0,16},{1,17},{2,18},{3,19},{4,20},{5,21},{6,22},{7,23},{8,24},{9,... | collective-permute-start | bytes 786440 | tf_op jit(solution)/shard_map/ppermute | solution.py:27

commit v2 on v1

--- a/solution.py
+++ b/solution.py
@@ -190,7 +190,6 @@
         in_specs=[pl.BlockSpec(memory_space=pl.ANY) for _ in operands],
         out_specs=tuple(pl.BlockSpec(memory_space=pltpu.VMEM) for _ in operands),
         scratch_shapes=[pltpu.SemaphoreType.DMA((len(operands),))],
-        name="stage",
         compiler_params=pltpu.CompilerParams(vmem_limit_bytes=GRANT),
     )(*operands)
 
@@ -203,9 +202,13 @@
     return call(mark_body, [((8, 128), jnp.float32)], [block])
 
 
-def fourth_body(assign_ref, root_ref, early_ref, late_ref, out_ref):
+def squared_body(root_ref, out_ref):
     value = split(root_ref[...])
-    value = split(multiply(value, value))
+    out_ref[...] = multiply(value, value)
+
+
+def fourth_body(assign_ref, squared_ref, early_ref, out_ref):
+    value = split(squared_ref[...])
     out_ref[...] = multiply(value, value)
 
 
@@ -337,12 +340,14 @@
     parts = {}
     for mask in reversed([2] + far):
         parts[mask] = moved(sent, "blk", mask)
-    parts[0], grad, warm, stat = stage([sent, grad_out, root_old[0, 0], stat_old[0, 0]])
+    parts[0], grad, warm = stage([sent, grad_out, root_old[0, 0]])
+    (stat,) = stage([stat_old[0, 0]])
     for mask in far:
         parts[mask | 2] = moved(parts[mask], "blk", 2)
     grads = [grad, moved(grad_out, "blk", 1)]
-    marks = mark(parts[0]) + mark(grads[0])
-    (fourth,) = call(fourth_body, [(square, jnp.float32)], [assign, warm, *marks])
+    early = mark(parts[0])
+    (squared,) = call(squared_body, [(square, jnp.float32)], [warm])
+    (fourth,) = call(fourth_body, [(square, jnp.float32)], [assign, squared, *early])
     groups = []
     operands = [assign]
     for masks in ([0, 2] + far[:1], far[1:] + [far[0] | 2], [mask | 2 for mask in far[1:]]):

time: 60.2 us -> 60.3 us (level)
  Pallas kernels: 16.9 us -> 17.9 us
  local copies, waits for them, and re-layouts: 2.36 us -> 1.71 us
    pallas_call x1 -> x2, Pallas kernels: 1.93 us -> 2.84 us  [stage(): pl.pallas_call(stage_body, out_shape=tuple((pltpu.VMEM(operand.shape, ope...]
    ppermute x8, waiting for transfers between devices: 15.8 us -> 15.1 us  [crossed(): lax.ppermute(block, ('tok', 'blk'), [(low, low ^ half ^ mask) for low in...]
    unnamed x5, local copies, waits for them, and re-layouts: 2.36 us -> 1.71 us
  transfers between devices with their start and end apart: 19 -> 19, of which waited for: 7 -> 7; matrix products, arithmetic and copies ran while one was open for 2% -> 2% of each run, Pallas kernels for 12% -> 13%
where the time goes in v2:
time: 60.3 us; the launch traced here: 60 us
  waiting for transfers between devices  20.8 us (34%)
  starting transfers between devices  18.3 us (30%)
  Pallas kernels  17.9 us (30%)
  local copies, waits for them, and re-layouts  1.71 us (3%)
  between operations  0.92 us (2%)
    pallas_call x10, Pallas kernels, call(): pl.pallas_call(body, out_shape=tuple(((pltpu.VMEM if kept else jax.ShapeD...  15.1 us
    ppermute x8, waiting for transfers between devices, crossed(): lax.ppermute(block, ('tok', 'blk'), [(low, low ^ half ^ mask) for low in...  15.1 us
    ppermute x11, starting transfers between devices, moved(): lax.ppermute(block, axis, [(low, low ^ mask) for low in range(count) if l...  11 us
    ppermute x8, starting transfers between devices, crossed(): lax.ppermute(block, ('tok', 'blk'), [(low, low ^ half ^ mask) for low in...  7.37 us
    ppermute x11, waiting for transfers between devices, moved(): lax.ppermute(block, axis, [(low, low ^ mask) for low in range(count) if l...  5.71 us
    pallas_call x2, Pallas kernels, stage(): pl.pallas_call(stage_body, out_shape=tuple((pltpu.VMEM(operand.shape, ope...  2.84 us
    unnamed x5, local copies, waits for them, and re-layouts  1.71 us
  transfers between devices with their start and end apart: 19, of which 7 were waited for; matrix products, arithmetic and copies ran while one was open for 2% of the time, Pallas kernels for 13%

profile of v2, /device:TPU:0, one launch (start us, length us, event | category | flops | bytes accessed | tf_op | source)
XLA Modules:
  0.0 60.0 jit_solution(8070687601326185910)
XLA Ops:
  0.6 0.6 collective-permute-start.2
  1.2 4.7 %collective-permute-start.7 = (bf16[32,1024]{1,0:T(8,128)(2,1)}, bf16[32,1024]{1,0:T(8,128)(2,1)S(1)}, u32[]{:S(2)}, u32[]{:S(2)}) collective-permute-start(bf16[32,1024]{1,0:T(8,128)(2,1)} %bitcast.9), channel_id=1, source_target_pairs={{0,12},{1,13},{2,14},{3,15},{4,8},{5,9},{6,10},{7,11},{8,4},{9,5},... | collective-permute-start | bytes 196616 | tf_op jit(solution)/shard_map/ppermute | solution.py:34
  5.9 0.6 %collective-permute-start.1 = (bf16[32,1024]{1,0:T(8,128)(2,1)}, bf16[32,1024]{1,0:T(8,128)(2,1)S(1)}, u32[]{:S(2)}, u32[]{:S(2)}) collective-permute-start(bf16[32,1024]{1,0:T(8,128)(2,1)} %bitcast.11), channel_id=1, source_target_pairs={{0,4},{1,5},{2,6},{3,7},{4,0},{5,1},{6,2},{7,3},{8,12},{9,13},{10,... | collective-permute-start | bytes 196616 | tf_op jit(solution)/shard_map/ppermute | solution.py:34
  6.5 2.5 %collective-permute-done.7.refs_1_ = bf16[32,1024]{1,0:T(8,128)(2,1)S(1)} collective-permute-done((bf16[32,1024]{1,0:T(8,128)(2,1)}, bf16[32,1024]{1,0:T(8,128)(2,1)S(1)}, u32[]{:S(2)}, u32[]{:S(2)}) %collective-permute-start.7) | collective-permute-done | bytes 65568 | tf_op jit(solution)/shard_map/ppermute | solution.py:34
  9.0 1.5 %collective-permute-start.13 = (bf16[32,1024]{1,0:T(8,128)(2,1)S(1)}, bf16[32,1024]{1,0:T(8,128)(2,1)S(1)}, u32[]{:S(2)}, u32[]{:S(2)}) collective-permute-start(bf16[32,1024]{1,0:T(8,128)(2,1)S(1)} %collective-permute-done.7.refs_1_), channel_id=1, source_target_pairs={{0,2},{1,3},{2,0},{3,1},{4,6},{5,7},{6,4},{7,5},{8,10},{9,11},{10,... | collective-permute-start | bytes 196616 | tf_op jit(solution)/shard_map/ppermute | solution.py:34
  10.5 1.6 %collective-permute-done.6.refs_0_ = bf16[32,1024]{1,0:T(8,128)(2,1)S(1)} collective-permute-done((bf16[32,1024]{1,0:T(8,128)(2,1)}, bf16[32,1024]{1,0:T(8,128)(2,1)S(1)}, u32[]{:S(2)}, u32[]{:S(2)}) %collective-permute-start.6) | collective-permute-done | bytes 65568 | tf_op jit(solution)/shard_map/ppermute | solution.py:34
  12.1 1.5 %collective-permute-start.12 = (bf16[32,1024]{1,0:T(8,128)(2,1)S(1)}, bf16[32,1024]{1,0:T(8,128)(2,1)S(1)}, u32[]{:S(2)}, u32[]{:S(2)}) collective-permute-start(bf16[32,1024]{1,0:T(8,128)(2,1)S(1)} %collective-permute-done.6.refs_0_), channel_id=1, source_target_pairs={{0,2},{1,3},{2,0},{3,1},{4,6},{5,7},{6,4},{7,5},{8,10},{9,11},{10,... | collective-permute-start | bytes 196616 | tf_op jit(solution)/shard_map/ppermute | solution.py:34
  13.6 0.5 collective-permute-start.8
  14.1 1.6 %shard_map.68 = (bf16[32,1024]{1,0:T(8,128)(2,1)S(1)}, bf16[1024,512]{1,0:T(8,128)(2,1)S(1)}, f32[512,512]{1,0:T(8,128)S(1)}) custom-call(bf16[32,1024]{1,0:T(8,128)(2,1)} %bitcast.12, bf16[1024,512]{1,0:T(8,128)(2,1)} %refs_1_.1, f32[512,512]{1,0:T(8,128)} %bitcast.6), custom_call_target="tpu_custom_call" | custom-call | tf_op jit(solution)/shard_map/pallas_call | solution.py:187
  15.8 1.2 %collective-permute-done.12.refs_0_ = bf16[32,1024]{1,0:T(8,128)(2,1)S(1)} collective-permute-done((bf16[32,1024]{1,0:T(8,128)(2,1)S(1)}, bf16[32,1024]{1,0:T(8,128)(2,1)S(1)}, u32[]{:S(2)}, u32[]{:S(2)}) %collective-permute-start.12) | collective-permute-done | bytes 65568 | tf_op jit(solution)/shard_map/ppermute | solution.py:34
  17.0 0.5 shard_map.71
  17.5 0.0 copy-start.1
  17.6 0.1 collective-permute-start.16
  17.6 0.7 %copy-done.1 = bf16[1024,32]{0,1:T(8,128)(2,1)S(1)} copy-done((bf16[1024,32]{0,1:T(8,128)(2,1)S(1)}, bf16[1024,32]{0,1:T(8,128)(2,1)}, u32[]{:S(2)}) %copy-start.1) | copy-done | bytes 65560
  18.4 1.0 %collective-permute-start = (bf16[32,1024]{1,0:T(8,128)(2,1)S(1)}, bf16[32,1024]{1,0:T(8,128)(2,1)S(1)}, u32[]{:S(2)}, u32[]{:S(2)}) collective-permute-start(bf16[32,1024]{1,0:T(8,128)(2,1)S(1)} %bitcast.13), channel_id=1, source_target_pairs={{0,2},{1,3},{2,0},{3,1},{4,6},{5,7},{6,4},{7,5},{8,10},{9,11},{10,... | collective-permute-start | bytes 196616 | tf_op jit(solution)/shard_map/ppermute | solution.py:34
  19.4 0.0 collective-permute-done.8.refs_2_
  19.4 0.5 shard_map.70
  19.9 0.8 %collective-permute-start.11 = (f16[104,512]{1,0:T(8,128)(2,1)S(1)}, f16[104,512]{1,0:T(8,128)(2,1)S(1)}, u32[]{:S(2)}, u32[]{:S(2)}) collective-permute-start(f16[104,512]{1,0:T(8,128)(2,1)S(1)} %convert_element_type.54), channel_id=1, source_target_pairs={{0,17},{1,16},{2,19},{3,18},{4,21},{5,20},{6,23},{7,22},{8,25},{9,... | collective-permute-start | bytes 319496 | tf_op jit(solution)/shard_map/ppermute | solution.py:27
  20.7 1.6 %collective-permute-start.9 = (f16[104,512]{1,0:T(8,128)(2,1)S(1)}, f16[104,512]{1,0:T(8,128)(2,1)S(1)}, u32[]{:S(2)}, u32[]{:S(2)}) collective-permute-start(f16[104,512]{1,0:T(8,128)(2,1)S(1)} %convert_element_type.52), channel_id=1, source_target_pairs={{0,16},{1,17},{2,18},{3,19},{4,20},{5,21},{6,22},{7,23},{8,24},{9,... | collective-permute-start | bytes 319496 | tf_op jit(solution)/shard_map/ppermute | solution.py:27
  22.3 0.6 collective-permute-start.14
  22.9 0.4 collective-permute-done.refs_1_
  23.2 0.5 shard_map.69
  23.8 0.1 collective-permute-start.4
  23.8 0.0 collective-permute-done.16
  23.8 0.5 collective-permute-start.10
  24.3 4.8 %collective-permute-done.14 = f16[72,512]{1,0:T(8,128)(2,1)S(1)} collective-permute-done((f16[72,512]{1,0:T(8,128)(2,1)S(1)}, f16[72,512]{1,0:T(8,128)(2,1)S(1)}, u32[]{:S(2)}, u32[]{:S(2)}) %collective-permute-start.14) | collective-permute-done | bytes 73760 | tf_op jit(solution)/shard_map/ppermute | solution.py:27
  29.1 0.0 collective-permute-start.15
  29.2 0.0 collective-permute-done.11
  29.2 1.3 %collective-permute-start.5 = (f16[104,512]{1,0:T(8,128)(2,1)S(1)}, f16[104,512]{1,0:T(8,128)(2,1)S(1)}, u32[]{:S(2)}, u32[]{:S(2)}) collective-permute-start(f16[104,512]{1,0:T(8,128)(2,1)S(1)} %convert_element_type.50), channel_id=1, source_target_pairs={{0,17},{1,16},{2,19},{3,18},{4,21},{5,20},{6,23},{7,22},{8,25},{9,... | collective-permute-start | bytes 319496 | tf_op jit(solution)/shard_map/ppermute | solution.py:27
  30.4 0.9 %collective-permute-start.3 = (f16[104,512]{1,0:T(8,128)(2,1)S(1)}, f16[104,512]{1,0:T(8,128)(2,1)S(1)}, u32[]{:S(2)}, u32[]{:S(2)}) collective-permute-start(f16[104,512]{1,0:T(8,128)(2,1)S(1)} %convert_element_type.48), channel_id=1, source_target_pairs={{0,16},{1,17},{2,18},{3,19},{4,20},{5,21},{6,22},{7,23},{8,24},{9,... | collective-permute-start | bytes 319496 | tf_op jit(solution)/shard_map/ppermute | solution.py:27
  31.4 1.2 %shard_map.72.refs_13_ = f32[512,512]{1,0:T(8,128)S(1)} custom-call(f32[512,512]{1,0:T(8,128)} %bitcast.7), custom_call_target="tpu_custom_call" | custom-call | tf_op jit(solution)/shard_map/pallas_call | solution.py:187
  32.6 0.0 copy-start
  32.6 1.0 %shard_map.73.squared_ref = f32[512,512]{1,0:T(8,128)S(1)} custom-call(f32[512,512]{1,0:T(8,128)S(1)} %get-tuple-element.38.root_ref.refs_14_), custom_call_target="tpu_custom_call" | custom-call | tf_op jit(solution)/shard_map/pallas_call | solution.py:322
  33.6 1.5 %shard_map.75.refs_15_ = f32[512,512]{1,0:T(8,128)S(1)} custom-call(s32[1,2]{1,0:T(1,128)S(1)} %copy-done, f32[512,512]{1,0:T(8,128)S(1)} %shard_map.73.squared_ref, f32[8,128]{1,0:T(8,128)S(1)} %shard_map.74.early_ref), custom_call_target="tpu_custom_call" | custom-call | tf_op jit(solution)/shard_map/pallas_call | solution.py:322
  35.2 0.0 collective-permute-done.5
  35.3 1.5 %collective-permute-done.3 = f16[104,512]{1,0:T(8,128)(2,1)S(1)} collective-permute-done((f16[104,512]{1,0:T(8,128)(2,1)S(1)}, f16[104,512]{1,0:T(8,128)(2,1)S(1)}, u32[]{:S(2)}, u32[]{:S(2)}) %collective-permute-start.3) | collective-permute-done | bytes 106528 | tf_op jit(solution)/shard_map/ppermute | solution.py:27
  36.8 0.0 collective-permute-done.4.refs_3_
  36.8 0.0 collective-permute-done.10.refs_7_
  36.8 7.1 %shard_map.76 = (f32[512,512]{1,0:T(8,128)S(1)}, f32[256,512]{1,0:T(8,128)S(1)}, f32[264,512]{1,0:T(8,128)S(1)}, bf16[512,512]{1,0:T(8,128)(2,1)S(1)}, bf16[512,512]{1,0:T(8,128)(2,1)S(1)}) custom-call(s32[1,2]{1,0:T(1,128)S(1)} %copy-done, f32[96,512]{1,0:T(8,128)S(1)} %get-tuple-element.26.refs_1_, f32[104,512]{1,0:T(8,128)S(1)} %convert_element_type.49.refs_2_, ...), custom_call_target="tpu_custom_call" | custom-call | tf_op jit(solution)/shard_map/pallas_call | solution.py:322
  43.9 0.9 %collective-permute-start.18 = (f16[264,512]{1,0:T(8,128)(2,1)S(1)}, f16[264,512]{1,0:T(8,128)(2,1)S(1)}, u32[]{:S(2)}, u32[]{:S(2)}) collective-permute-start(f16[264,512]{1,0:T(8,128)(2,1)S(1)} %convert_element_type.62), channel_id=1, source_target_pairs={{0,16},{1,17},{2,18},{3,19},{4,20},{5,21},{6,22},{7,23},{8,24},{9,... | collective-permute-start | bytes 811016 | tf_op jit(solution)/shard_map/ppermute | solution.py:27
  44.9 1.2 %collective-permute-start.17 = (f16[256,512]{1,0:T(8,128)(2,1)S(1)}, f16[256,512]{1,0:T(8,128)(2,1)S(1)}, u32[]{:S(2)}, u32[]{:S(2)}) collective-permute-start(f16[256,512]{1,0:T(8,128)(2,1)S(1)} %convert_element_type.60), channel_id=1, source_target_pairs={{0,16},{1,17},{2,18},{3,19},{4,20},{5,21},{6,22},{7,23},{8,24},{9,... | collective-permute-start | bytes 786440 | tf_op jit(solution)/shard_map/ppermute | solution.py:27
  46.1 1.0 %copy.7 = f32[1,1,512,512]{3,2,1,0:T(8,128)} copy(f32[1,1,512,512]{3,2,1,0:T(8,128)S(1)} %bitcast.5) | data formatting | bytes 2097152
  47.1 1.2 %shard_map.77.middle_ref = f32[512,512]{1,0:T(8,128)S(1)} custom-call(s32[1,2]{1,0:T(1,128)S(1)} %copy-done, f32[512,512]{1,0:T(8,128)S(1)} %get-tuple-element.39.root_ref, bf16[512,512]{1,0:T(8,128)(2,1)S(1)} %get-tuple-element.42.high_ref, bf16[512,512]{1,0:T(8,128)(2,1)S(1)} %get-tuple-element.43.low_ref), custom_call_target="tpu_custom_call" | custom-call | tf_op jit(solution)/shard_map/pallas_call | solution.py:322
  48.3 8.8 %collective-permute-done.17 = f16[256,512]{1,0:T(8,128)(2,1)S(1)} collective-permute-done((f16[256,512]{1,0:T(8,128)(2,1)S(1)}, f16[256,512]{1,0:T(8,128)(2,1)S(1)}, u32[]{:S(2)}, u32[]{:S(2)}) %collective-permute-start.17) | collective-permute-done | bytes 262176 | tf_op jit(solution)/shard_map/ppermute | solution.py:27
  57.1 0.1 convert_element_type.61.got_ref
  57.2 0.1 convert_element_type.63.got_ref
  57.2 1.0 %shard_map.78 = (f32[256,512]{1,0:T(8,128)S(1)}, f32[8,512]{1,0:T(8,128)S(1)}) custom-call(s32[1,2]{1,0:T(1,128)S(1)} %copy-done, f32[264,512]{1,0:T(8,128)S(1)} %convert_element_type.63.got_ref, f32[512,512]{1,0:T(8,128)S(1)} %shard_map.77.middle_ref), custom_call_target="tpu_custom_call" | custom-call | tf_op jit(solution)/shard_map/pallas_call | solution.py:322
  58.3 1.8 %shard_map.79 = f32[256,512]{1,0:T(8,128)} custom-call(s32[1,2]{1,0:T(1,128)S(1)} %copy-done, f32[256,512]{1,0:T(8,128)S(1)} %convert_element_type.61.got_ref, f32[8,512]{1,0:T(8,128)S(1)} %get-tuple-element.44.tail_ref, f32[512,512]{1,0:T(8,128)S(1)} %shard_map.77.middle_ref, f32[256,512]{1,0:T(8,128)S(1)} %get-tuple-element.45.begun_ref), custom_call_target="tpu_custom_call" | custom-call | tf_op jit(solution)/shard_map/pallas_call | solution.py:322
  (23 shorter events, 0.3 us)
Async XLA Ops:
  0.6 16.4 %collective-permute-start.2 = (bf16[1024,512]{1,0:T(8,128)(2,1)}, bf16[1024,512]{1,0:T(8,128)(2,1)S(1)}, u32[]{:S(2)}, u32[]{:S(2)}) collective-permute-start(bf16[1024,512]{1,0:T(8,128)(2,1)} %refs_1_.1), channel_id=1, source_target_pairs={{0,1},{1,0},{2,3},{3,2},{4,5},{5,4},{6,7},{7,6},{8,9},{9,8},{10,11... | collective-permute-start | bytes 3145736 | tf_op jit(solution)/shard_map/ppermute | solution.py:34
  1.2 7.8 %collective-permute-start.7 = (bf16[32,1024]{1,0:T(8,128)(2,1)}, bf16[32,1024]{1,0:T(8,128)(2,1)S(1)}, u32[]{:S(2)}, u32[]{:S(2)}) collective-permute-start(bf16[32,1024]{1,0:T(8,128)(2,1)} %bitcast.9), channel_id=1, source_target_pairs={{0,12},{1,13},{2,14},{3,15},{4,8},{5,9},{6,10},{7,11},{8,4},{9,5},... | collective-permute-start | bytes 196616 | tf_op jit(solution)/shard_map/ppermute | solution.py:34
  5.9 6.3 %collective-permute-start.6 = (bf16[32,1024]{1,0:T(8,128)(2,1)}, bf16[32,1024]{1,0:T(8,128)(2,1)S(1)}, u32[]{:S(2)}, u32[]{:S(2)}) collective-permute-start(bf16[32,1024]{1,0:T(8,128)(2,1)} %bitcast.10), channel_id=1, source_target_pairs={{0,8},{1,9},{2,10},{3,11},{4,12},{5,13},{6,14},{7,15},{8,0},{9,1},... | collective-permute-start | bytes 196616 | tf_op jit(solution)/shard_map/ppermute | solution.py:34
  5.9 7.8 %collective-permute-start.1 = (bf16[32,1024]{1,0:T(8,128)(2,1)}, bf16[32,1024]{1,0:T(8,128)(2,1)S(1)}, u32[]{:S(2)}, u32[]{:S(2)}) collective-permute-start(bf16[32,1024]{1,0:T(8,128)(2,1)} %bitcast.11), channel_id=1, source_target_pairs={{0,4},{1,5},{2,6},{3,7},{4,0},{5,1},{6,2},{7,3},{8,12},{9,13},{10,... | collective-permute-start | bytes 196616 | tf_op jit(solution)/shard_map/ppermute | solution.py:34
  9.0 6.8 %collective-permute-start.13 = (bf16[32,1024]{1,0:T(8,128)(2,1)S(1)}, bf16[32,1024]{1,0:T(8,128)(2,1)S(1)}, u32[]{:S(2)}, u32[]{:S(2)}) collective-permute-start(bf16[32,1024]{1,0:T(8,128)(2,1)S(1)} %collective-permute-done.7.refs_1_), channel_id=1, source_target_pairs={{0,2},{1,3},{2,0},{3,1},{4,6},{5,7},{6,4},{7,5},{8,10},{9,11},{10,... | collective-permute-start | bytes 196616 | tf_op jit(solution)/shard_map/ppermute | solution.py:34
  12.1 4.9 %collective-permute-start.12 = (bf16[32,1024]{1,0:T(8,128)(2,1)S(1)}, bf16[32,1024]{1,0:T(8,128)(2,1)S(1)}, u32[]{:S(2)}, u32[]{:S(2)}) collective-permute-start(bf16[32,1024]{1,0:T(8,128)(2,1)S(1)} %collective-permute-done.6.refs_0_), channel_id=1, source_target_pairs={{0,2},{1,3},{2,0},{3,1},{4,6},{5,7},{6,4},{7,5},{8,10},{9,11},{10,... | collective-permute-start | bytes 196616 | tf_op jit(solution)/shard_map/ppermute | solution.py:34
  13.6 5.7 %collective-permute-start.8 = (bf16[32,1024]{1,0:T(8,128)(2,1)S(1)}, bf16[32,1024]{1,0:T(8,128)(2,1)S(1)}, u32[]{:S(2)}, u32[]{:S(2)}) collective-permute-start(bf16[32,1024]{1,0:T(8,128)(2,1)S(1)} %collective-permute-done.1.refs_2_), channel_id=1, source_target_pairs={{0,2},{1,3},{2,0},{3,1},{4,6},{5,7},{6,4},{7,5},{8,10},{9,11},{10,... | collective-permute-start | bytes 196616 | tf_op jit(solution)/shard_map/ppermute | solution.py:34
  17.5 0.8 %copy-start.1 = (bf16[1024,32]{0,1:T(8,128)(2,1)S(1)}, bf16[1024,32]{0,1:T(8,128)(2,1)}, u32[]{:S(2)}) copy-start(bf16[1024,32]{0,1:T(8,128)(2,1)} %param.6) | copy-start | bytes 196612
  17.6 6.3 %collective-permute-start.16 = (f16[72,512]{1,0:T(8,128)(2,1)S(1)}, f16[72,512]{1,0:T(8,128)(2,1)S(1)}, u32[]{:S(2)}, u32[]{:S(2)}) collective-permute-start(f16[72,512]{1,0:T(8,128)(2,1)S(1)} %convert_element_type.58), channel_id=1, source_target_pairs={{0,17},{1,16},{2,19},{3,18},{4,21},{5,20},{6,23},{7,22},{8,25},{9,... | collective-permute-start | bytes 221192 | tf_op jit(solution)/shard_map/ppermute | solution.py:27
  18.4 4.9 %collective-permute-start = (bf16[32,1024]{1,0:T(8,128)(2,1)S(1)}, bf16[32,1024]{1,0:T(8,128)(2,1)S(1)}, u32[]{:S(2)}, u32[]{:S(2)}) collective-permute-start(bf16[32,1024]{1,0:T(8,128)(2,1)S(1)} %bitcast.13), channel_id=1, source_target_pairs={{0,2},{1,3},{2,0},{3,1},{4,6},{5,7},{6,4},{7,5},{8,10},{9,11},{10,... | collective-permute-start | bytes 196616 | tf_op jit(solution)/shard_map/ppermute | solution.py:34
  19.9 9.2 %collective-permute-start.11 = (f16[104,512]{1,0:T(8,128)(2,1)S(1)}, f16[104,512]{1,0:T(8,128)(2,1)S(1)}, u32[]{:S(2)}, u32[]{:S(2)}) collective-permute-start(f16[104,512]{1,0:T(8,128)(2,1)S(1)} %convert_element_type.54), channel_id=1, source_target_pairs={{0,17},{1,16},{2,19},{3,18},{4,21},{5,20},{6,23},{7,22},{8,25},{9,... | collective-permute-start | bytes 319496 | tf_op jit(solution)/shard_map/ppermute | solution.py:27
  20.7 9.7 %collective-permute-start.9 = (f16[104,512]{1,0:T(8,128)(2,1)S(1)}, f16[104,512]{1,0:T(8,128)(2,1)S(1)}, u32[]{:S(2)}, u32[]{:S(2)}) collective-permute-start(f16[104,512]{1,0:T(8,128)(2,1)S(1)} %convert_element_type.52), channel_id=1, source_target_pairs={{0,16},{1,17},{2,18},{3,19},{4,20},{5,21},{6,22},{7,23},{8,24},{9,... | collective-permute-start | bytes 319496 | tf_op jit(solution)/shard_map/ppermute | solution.py:27
  22.3 6.8 %collective-permute-start.14 = (f16[72,512]{1,0:T(8,128)(2,1)S(1)}, f16[72,512]{1,0:T(8,128)(2,1)S(1)}, u32[]{:S(2)}, u32[]{:S(2)}) collective-permute-start(f16[72,512]{1,0:T(8,128)(2,1)S(1)} %convert_element_type.56), channel_id=1, source_target_pairs={{0,16},{1,17},{2,18},{3,19},{4,20},{5,21},{6,22},{7,23},{8,24},{9,... | collective-permute-start | bytes 221192 | tf_op jit(solution)/shard_map/ppermute | solution.py:27
  23.8 13.1 %collective-permute-start.4 = (f32[96,512]{1,0:T(8,128)S(1)}, f32[96,512]{1,0:T(8,128)S(1)}, u32[]{:S(2)}, u32[]{:S(2)}) collective-permute-start(f32[96,512]{1,0:T(8,128)S(1)} %get-tuple-element.28), channel_id=1, source_target_pairs={{0,1},{1,0},{2,3},{3,2},{4,5},{5,4},{6,7},{7,6},{8,9},{9,8},{10,11... | collective-permute-start | bytes 589832 | tf_op jit(solution)/shard_map/ppermute | solution.py:34
  23.8 13.0 %collective-permute-start.10 = (f32[96,512]{1,0:T(8,128)S(1)}, f32[96,512]{1,0:T(8,128)S(1)}, u32[]{:S(2)}, u32[]{:S(2)}) collective-permute-start(f32[96,512]{1,0:T(8,128)S(1)} %get-tuple-element.32), channel_id=1, source_target_pairs={{0,1},{1,0},{2,3},{3,2},{4,5},{5,4},{6,7},{7,6},{8,9},{9,8},{10,11... | collective-permute-start | bytes 589832 | tf_op jit(solution)/shard_map/ppermute | solution.py:34
  29.1 7.7 %collective-permute-start.15 = (f32[64,512]{1,0:T(8,128)S(1)}, f32[64,512]{1,0:T(8,128)S(1)}, u32[]{:S(2)}, u32[]{:S(2)}) collective-permute-start(f32[64,512]{1,0:T(8,128)S(1)} %get-tuple-element.36), channel_id=1, source_target_pairs={{0,1},{1,0},{2,3},{3,2},{4,5},{5,4},{6,7},{7,6},{8,9},{9,8},{10,11... | collective-permute-start | bytes 393224 | tf_op jit(solution)/shard_map/ppermute | solution.py:34
  29.2 6.1 %collective-permute-start.5 = (f16[104,512]{1,0:T(8,128)(2,1)S(1)}, f16[104,512]{1,0:T(8,128)(2,1)S(1)}, u32[]{:S(2)}, u32[]{:S(2)}) collective-permute-start(f16[104,512]{1,0:T(8,128)(2,1)S(1)} %convert_element_type.50), channel_id=1, source_target_pairs={{0,17},{1,16},{2,19},{3,18},{4,21},{5,20},{6,23},{7,22},{8,25},{9,... | collective-permute-start | bytes 319496 | tf_op jit(solution)/shard_map/ppermute | solution.py:27
  30.4 6.3 %collective-permute-start.3 = (f16[104,512]{1,0:T(8,128)(2,1)S(1)}, f16[104,512]{1,0:T(8,128)(2,1)S(1)}, u32[]{:S(2)}, u32[]{:S(2)}) collective-permute-start(f16[104,512]{1,0:T(8,128)(2,1)S(1)} %convert_element_type.48), channel_id=1, source_target_pairs={{0,16},{1,17},{2,18},{3,19},{4,20},{5,21},{6,22},{7,23},{8,24},{9,... | collective-permute-start | bytes 319496 | tf_op jit(solution)/shard_map/ppermute | solution.py:27
  32.6 1.0 %copy-start = (s32[1,2]{1,0:T(1,128)S(1)}, s32[1,2]{1,0:T(1,128)}, u32[]{:S(2)}) copy-start(s32[1,2]{1,0:T(1,128)} %assign_ref.7) | copy-start | bytes 28
  43.9 13.2 %collective-permute-start.18 = (f16[264,512]{1,0:T(8,128)(2,1)S(1)}, f16[264,512]{1,0:T(8,128)(2,1)S(1)}, u32[]{:S(2)}, u32[]{:S(2)}) collective-permute-start(f16[264,512]{1,0:T(8,128)(2,1)S(1)} %convert_element_type.62), channel_id=1, source_target_pairs={{0,16},{1,17},{2,18},{3,19},{4,20},{5,21},{6,22},{7,23},{8,24},{9,... | collective-permute-start | bytes 811016 | tf_op jit(solution)/shard_map/ppermute | solution.py:27
  44.9 12.2 %collective-permute-start.17 = (f16[256,512]{1,0:T(8,128)(2,1)S(1)}, f16[256,512]{1,0:T(8,128)(2,1)S(1)}, u32[]{:S(2)}, u32[]{:S(2)}) collective-permute-start(f16[256,512]{1,0:T(8,128)(2,1)S(1)} %convert_element_type.60), channel_id=1, source_target_pairs={{0,16},{1,17},{2,18},{3,19},{4,20},{5,21},{6,22},{7,23},{8,24},{9,... | collective-permute-start | bytes 786440 | tf_op jit(solution)/shard_map/ppermute | solution.py:27

commit v3 on v2

--- a/solution.py
+++ b/solution.py
@@ -262,18 +262,22 @@
     bottom_ref[half:, :] = tail
 
 
-def middle_body(assign_ref, root_ref, high_ref, low_ref, out_ref):
+def middle_body(assign_ref, root_ref, high_ref, low_ref, out_high_ref, out_low_ref):
     half = root_ref.shape[0] // 2
     oriented = high_ref[...], low_ref[...]
 
     @pl.when(side_of(assign_ref) == 0)
     def _():
-        out_ref[0:half, :] = multiply(split(root_ref[0:half, :]), oriented)
-        out_ref[half:, :] = jnp.zeros((half, root_ref.shape[1]), jnp.float32)
+        held = split(multiply(split(root_ref[0:half, :]), oriented))
+        out_high_ref[0:half, :], out_low_ref[0:half, :] = held
+        out_high_ref[half:, :] = jnp.zeros((half, root_ref.shape[1]), jnp.bfloat16)
+        out_low_ref[half:, :] = jnp.zeros((half, root_ref.shape[1]), jnp.bfloat16)
 
     @pl.when(side_of(assign_ref) != 0)
     def _():
-        out_ref[...] = multiply(oriented, split(root_ref[...]), ((0,), (0,)))
+        out_high_ref[...], out_low_ref[...] = split(
+            multiply(oriented, split(root_ref[...]), ((0,), (0,)))
+        )
 
 
 def decoded(rows, tail, offset):
@@ -283,28 +287,28 @@
     return jnp.where(mask, tail[1:2, :] + tail[2:3, :], rows) * jnp.exp2(tail[0:1, :])
 
 
-def bottom_body(assign_ref, got_ref, middle_ref, out_ref, tail_ref):
-    half = middle_ref.shape[0] // 2
+def bottom_body(assign_ref, got_ref, high_ref, low_ref, out_ref, tail_ref):
+    half = high_ref.shape[0] // 2
     tail = got_ref[half:, :]
     tail_ref[...] = tail
     other = split(decoded(got_ref[0:half, :], tail, half))
 
     @pl.when(side_of(assign_ref) == 0)
     def _():
-        out_ref[...] = multiply(split(middle_ref[0:half, half:]), other)
+        out_ref[...] = multiply((high_ref[0:half, half:], low_ref[0:half, half:]), other)
 
     @pl.when(side_of(assign_ref) != 0)
     def _():
-        out_ref[...] = multiply(other, split(middle_ref[...]))
-
-
-def top_body(assign_ref, got_ref, tail_ref, middle_ref, begun_ref, out_ref):
-    half = middle_ref.shape[0] // 2
+        out_ref[...] = multiply(other, (high_ref[...], low_ref[...]))
+
+
+def top_body(assign_ref, got_ref, tail_ref, high_ref, low_ref, begun_ref, out_ref):
+    half = high_ref.shape[0] // 2
 
     @pl.when(side_of(assign_ref) == 0)
     def _():
         other = split(decoded(got_ref[...], tail_ref[...], 0))
-        out_ref[...] = begun_ref[...] + multiply(split(middle_ref[0:half, 0:half]), other)
+        out_ref[...] = begun_ref[...] + multiply((high_ref[0:half, 0:half], low_ref[0:half, 0:half]), other)
 
     @pl.when(side_of(assign_ref) != 0)
     def _():
@@ -374,16 +378,16 @@
     )
     bottom = crossed(bottom.astype(jnp.float16), 0)
     top = crossed(top.astype(jnp.float16), 0)
-    (middle,) = call(middle_body, [(square, jnp.float32)], [assign, own_root, high, low])
+    middle = call(middle_body, [(square, jnp.bfloat16)] * 2, [assign, own_root, high, low])
     begun, tail = call(
         bottom_body,
         [((half, size), jnp.float32), ((TAIL, size), jnp.float32)],
-        [assign, bottom.astype(jnp.float32), middle],
+        [assign, bottom.astype(jnp.float32), *middle],
     )
     (precond,) = call(
         top_body,
         [((half, size), jnp.float32)],
-        [assign, top.astype(jnp.float32), tail, middle, begun],
+        [assign, top.astype(jnp.float32), tail, *middle, begun],
         kept=False,
     )
     return (own_root[None, None], precond[None, None])

time: 60.3 us -> 60.3 us (level)
  no operation moved by 1% of the time
where the time goes in v3:
time: 60.3 us; the launch traced here: 60 us
  waiting for transfers between devices  20.8 us (34%)
  starting transfers between devices  18.3 us (30%)
  Pallas kernels  17.9 us (30%)
  local copies, waits for them, and re-layouts  1.71 us (3%)
  between operations  0.92 us (2%)
    pallas_call x10, Pallas kernels, call(): pl.pallas_call(body, out_shape=tuple(((pltpu.VMEM if kept else jax.ShapeD...  15.1 us
    ppermute x8, waiting for transfers between devices, crossed(): lax.ppermute(block, ('tok', 'blk'), [(low, low ^ half ^ mask) for low in...  15.1 us
    ppermute x11, starting transfers between devices, moved(): lax.ppermute(block, axis, [(low, low ^ mask) for low in range(count) if l...  11 us
    ppermute x8, starting transfers between devices, crossed(): lax.ppermute(block, ('tok', 'blk'), [(low, low ^ half ^ mask) for low in...  7.37 us
    ppermute x11, waiting for transfers between devices, moved(): lax.ppermute(block, axis, [(low, low ^ mask) for low in range(count) if l...  5.71 us
    pallas_call x2, Pallas kernels, stage(): pl.pallas_call(stage_body, out_shape=tuple((pltpu.VMEM(operand.shape, ope...  2.84 us
    unnamed x5, local copies, waits for them, and re-layouts  1.71 us
  transfers between devices with their start and end apart: 19, of which 7 were waited for; matrix products, arithmetic and copies ran while one was open for 2% of the time, Pallas kernels for 13%

profile of v3, /device:TPU:0, one launch (start us, length us, event | category | flops | bytes accessed | tf_op | source)
XLA Modules:
  0.0 60.0 jit_solution(5578592019138018545)
XLA Ops:
  0.6 0.6 collective-permute-start.2
  1.2 4.7 %collective-permute-start.7 = (bf16[32,1024]{1,0:T(8,128)(2,1)}, bf16[32,1024]{1,0:T(8,128)(2,1)S(1)}, u32[]{:S(2)}, u32[]{:S(2)}) collective-permute-start(bf16[32,1024]{1,0:T(8,128)(2,1)} %bitcast.9), channel_id=1, source_target_pairs={{0,12},{1,13},{2,14},{3,15},{4,8},{5,9},{6,10},{7,11},{8,4},{9,5},... | collective-permute-start | bytes 196616 | tf_op jit(solution)/shard_map/ppermute | solution.py:34
  5.9 0.6 %collective-permute-start.1 = (bf16[32,1024]{1,0:T(8,128)(2,1)}, bf16[32,1024]{1,0:T(8,128)(2,1)S(1)}, u32[]{:S(2)}, u32[]{:S(2)}) collective-permute-start(bf16[32,1024]{1,0:T(8,128)(2,1)} %bitcast.11), channel_id=1, source_target_pairs={{0,4},{1,5},{2,6},{3,7},{4,0},{5,1},{6,2},{7,3},{8,12},{9,13},{10,... | collective-permute-start | bytes 196616 | tf_op jit(solution)/shard_map/ppermute | solution.py:34
  6.5 2.5 %collective-permute-done.7.refs_1_ = bf16[32,1024]{1,0:T(8,128)(2,1)S(1)} collective-permute-done((bf16[32,1024]{1,0:T(8,128)(2,1)}, bf16[32,1024]{1,0:T(8,128)(2,1)S(1)}, u32[]{:S(2)}, u32[]{:S(2)}) %collective-permute-start.7) | collective-permute-done | bytes 65568 | tf_op jit(solution)/shard_map/ppermute | solution.py:34
  9.0 1.5 %collective-permute-start.13 = (bf16[32,1024]{1,0:T(8,128)(2,1)S(1)}, bf16[32,1024]{1,0:T(8,128)(2,1)S(1)}, u32[]{:S(2)}, u32[]{:S(2)}) collective-permute-start(bf16[32,1024]{1,0:T(8,128)(2,1)S(1)} %collective-permute-done.7.refs_1_), channel_id=1, source_target_pairs={{0,2},{1,3},{2,0},{3,1},{4,6},{5,7},{6,4},{7,5},{8,10},{9,11},{10,... | collective-permute-start | bytes 196616 | tf_op jit(solution)/shard_map/ppermute | solution.py:34
  10.5 1.6 %collective-permute-done.6.refs_0_ = bf16[32,1024]{1,0:T(8,128)(2,1)S(1)} collective-permute-done((bf16[32,1024]{1,0:T(8,128)(2,1)}, bf16[32,1024]{1,0:T(8,128)(2,1)S(1)}, u32[]{:S(2)}, u32[]{:S(2)}) %collective-permute-start.6) | collective-permute-done | bytes 65568 | tf_op jit(solution)/shard_map/ppermute | solution.py:34
  12.1 1.5 %collective-permute-start.12 = (bf16[32,1024]{1,0:T(8,128)(2,1)S(1)}, bf16[32,1024]{1,0:T(8,128)(2,1)S(1)}, u32[]{:S(2)}, u32[]{:S(2)}) collective-permute-start(bf16[32,1024]{1,0:T(8,128)(2,1)S(1)} %collective-permute-done.6.refs_0_), channel_id=1, source_target_pairs={{0,2},{1,3},{2,0},{3,1},{4,6},{5,7},{6,4},{7,5},{8,10},{9,11},{10,... | collective-permute-start | bytes 196616 | tf_op jit(solution)/shard_map/ppermute | solution.py:34
  13.6 0.5 collective-permute-start.8
  14.1 1.6 %shard_map.68 = (bf16[32,1024]{1,0:T(8,128)(2,1)S(1)}, bf16[1024,512]{1,0:T(8,128)(2,1)S(1)}, f32[512,512]{1,0:T(8,128)S(1)}) custom-call(bf16[32,1024]{1,0:T(8,128)(2,1)} %bitcast.12, bf16[1024,512]{1,0:T(8,128)(2,1)} %refs_1_.1, f32[512,512]{1,0:T(8,128)} %bitcast.6), custom_call_target="tpu_custom_call" | custom-call | tf_op jit(solution)/shard_map/pallas_call | solution.py:187
  15.8 1.2 %collective-permute-done.12.refs_0_ = bf16[32,1024]{1,0:T(8,128)(2,1)S(1)} collective-permute-done((bf16[32,1024]{1,0:T(8,128)(2,1)S(1)}, bf16[32,1024]{1,0:T(8,128)(2,1)S(1)}, u32[]{:S(2)}, u32[]{:S(2)}) %collective-permute-start.12) | collective-permute-done | bytes 65568 | tf_op jit(solution)/shard_map/ppermute | solution.py:34
  17.0 0.5 shard_map.71
  17.5 0.0 copy-start.1
  17.6 0.1 collective-permute-start.16
  17.6 0.7 %copy-done.1 = bf16[1024,32]{0,1:T(8,128)(2,1)S(1)} copy-done((bf16[1024,32]{0,1:T(8,128)(2,1)S(1)}, bf16[1024,32]{0,1:T(8,128)(2,1)}, u32[]{:S(2)}) %copy-start.1) | copy-done | bytes 65560
  18.4 1.0 %collective-permute-start = (bf16[32,1024]{1,0:T(8,128)(2,1)S(1)}, bf16[32,1024]{1,0:T(8,128)(2,1)S(1)}, u32[]{:S(2)}, u32[]{:S(2)}) collective-permute-start(bf16[32,1024]{1,0:T(8,128)(2,1)S(1)} %bitcast.13), channel_id=1, source_target_pairs={{0,2},{1,3},{2,0},{3,1},{4,6},{5,7},{6,4},{7,5},{8,10},{9,11},{10,... | collective-permute-start | bytes 196616 | tf_op jit(solution)/shard_map/ppermute | solution.py:34
  19.4 0.0 collective-permute-done.8.refs_2_
  19.4 0.5 shard_map.70
  19.9 0.8 %collective-permute-start.11 = (f16[104,512]{1,0:T(8,128)(2,1)S(1)}, f16[104,512]{1,0:T(8,128)(2,1)S(1)}, u32[]{:S(2)}, u32[]{:S(2)}) collective-permute-start(f16[104,512]{1,0:T(8,128)(2,1)S(1)} %convert_element_type.54), channel_id=1, source_target_pairs={{0,17},{1,16},{2,19},{3,18},{4,21},{5,20},{6,23},{7,22},{8,25},{9,... | collective-permute-start | bytes 319496 | tf_op jit(solution)/shard_map/ppermute | solution.py:27
  20.7 1.6 %collective-permute-start.9 = (f16[104,512]{1,0:T(8,128)(2,1)S(1)}, f16[104,512]{1,0:T(8,128)(2,1)S(1)}, u32[]{:S(2)}, u32[]{:S(2)}) collective-permute-start(f16[104,512]{1,0:T(8,128)(2,1)S(1)} %convert_element_type.52), channel_id=1, source_target_pairs={{0,16},{1,17},{2,18},{3,19},{4,20},{5,21},{6,22},{7,23},{8,24},{9,... | collective-permute-start | bytes 319496 | tf_op jit(solution)/shard_map/ppermute | solution.py:27
  22.3 0.6 collective-permute-start.14
  22.9 0.4 collective-permute-done.refs_1_
  23.2 0.5 shard_map.69
  23.8 0.1 collective-permute-start.4
  23.8 0.0 collective-permute-done.16
  23.8 0.5 collective-permute-start.10
  24.3 4.8 %collective-permute-done.14 = f16[72,512]{1,0:T(8,128)(2,1)S(1)} collective-permute-done((f16[72,512]{1,0:T(8,128)(2,1)S(1)}, f16[72,512]{1,0:T(8,128)(2,1)S(1)}, u32[]{:S(2)}, u32[]{:S(2)}) %collective-permute-start.14) | collective-permute-done | bytes 73760 | tf_op jit(solution)/shard_map/ppermute | solution.py:27
  29.1 0.0 collective-permute-start.15
  29.2 0.0 collective-permute-done.11
  29.2 1.3 %collective-permute-start.5 = (f16[104,512]{1,0:T(8,128)(2,1)S(1)}, f16[104,512]{1,0:T(8,128)(2,1)S(1)}, u32[]{:S(2)}, u32[]{:S(2)}) collective-permute-start(f16[104,512]{1,0:T(8,128)(2,1)S(1)} %convert_element_type.50), channel_id=1, source_target_pairs={{0,17},{1,16},{2,19},{3,18},{4,21},{5,20},{6,23},{7,22},{8,25},{9,... | collective-permute-start | bytes 319496 | tf_op jit(solution)/shard_map/ppermute | solution.py:27
  30.4 0.9 %collective-permute-start.3 = (f16[104,512]{1,0:T(8,128)(2,1)S(1)}, f16[104,512]{1,0:T(8,128)(2,1)S(1)}, u32[]{:S(2)}, u32[]{:S(2)}) collective-permute-start(f16[104,512]{1,0:T(8,128)(2,1)S(1)} %convert_element_type.48), channel_id=1, source_target_pairs={{0,16},{1,17},{2,18},{3,19},{4,20},{5,21},{6,22},{7,23},{8,24},{9,... | collective-permute-start | bytes 319496 | tf_op jit(solution)/shard_map/ppermute | solution.py:27
  31.4 1.2 %shard_map.72.refs_13_ = f32[512,512]{1,0:T(8,128)S(1)} custom-call(f32[512,512]{1,0:T(8,128)} %bitcast.7), custom_call_target="tpu_custom_call" | custom-call | tf_op jit(solution)/shard_map/pallas_call | solution.py:187
  32.6 0.0 copy-start
  32.6 1.0 %shard_map.73.squared_ref = f32[512,512]{1,0:T(8,128)S(1)} custom-call(f32[512,512]{1,0:T(8,128)S(1)} %get-tuple-element.40.root_ref.refs_14_), custom_call_target="tpu_custom_call" | custom-call | tf_op jit(solution)/shard_map/pallas_call | solution.py:326
  33.6 1.5 %shard_map.75.refs_15_ = f32[512,512]{1,0:T(8,128)S(1)} custom-call(s32[1,2]{1,0:T(1,128)S(1)} %copy-done, f32[512,512]{1,0:T(8,128)S(1)} %shard_map.73.squared_ref, f32[8,128]{1,0:T(8,128)S(1)} %shard_map.74.early_ref), custom_call_target="tpu_custom_call" | custom-call | tf_op jit(solution)/shard_map/pallas_call | solution.py:326
  35.2 0.0 collective-permute-done.5
  35.3 1.5 %collective-permute-done.3 = f16[104,512]{1,0:T(8,128)(2,1)S(1)} collective-permute-done((f16[104,512]{1,0:T(8,128)(2,1)S(1)}, f16[104,512]{1,0:T(8,128)(2,1)S(1)}, u32[]{:S(2)}, u32[]{:S(2)}) %collective-permute-start.3) | collective-permute-done | bytes 106528 | tf_op jit(solution)/shard_map/ppermute | solution.py:27
  36.8 0.0 collective-permute-done.4.refs_3_
  36.8 0.0 collective-permute-done.10.refs_7_
  36.8 7.1 %shard_map.76 = (f32[512,512]{1,0:T(8,128)S(1)}, f32[256,512]{1,0:T(8,128)S(1)}, f32[264,512]{1,0:T(8,128)S(1)}, bf16[512,512]{1,0:T(8,128)(2,1)S(1)}, bf16[512,512]{1,0:T(8,128)(2,1)S(1)}) custom-call(s32[1,2]{1,0:T(1,128)S(1)} %copy-done, f32[96,512]{1,0:T(8,128)S(1)} %get-tuple-element.28.refs_1_, f32[104,512]{1,0:T(8,128)S(1)} %convert_element_type.49.refs_2_, ...), custom_call_target="tpu_custom_call" | custom-call | tf_op jit(solution)/shard_map/pallas_call | solution.py:326
  43.9 0.9 %collective-permute-start.18 = (f16[264,512]{1,0:T(8,128)(2,1)S(1)}, f16[264,512]{1,0:T(8,128)(2,1)S(1)}, u32[]{:S(2)}, u32[]{:S(2)}) collective-permute-start(f16[264,512]{1,0:T(8,128)(2,1)S(1)} %convert_element_type.62), channel_id=1, source_target_pairs={{0,16},{1,17},{2,18},{3,19},{4,20},{5,21},{6,22},{7,23},{8,24},{9,... | collective-permute-start | bytes 811016 | tf_op jit(solution)/shard_map/ppermute | solution.py:27
  44.9 1.2 %collective-permute-start.17 = (f16[256,512]{1,0:T(8,128)(2,1)S(1)}, f16[256,512]{1,0:T(8,128)(2,1)S(1)}, u32[]{:S(2)}, u32[]{:S(2)}) collective-permute-start(f16[256,512]{1,0:T(8,128)(2,1)S(1)} %convert_element_type.60), channel_id=1, source_target_pairs={{0,16},{1,17},{2,18},{3,19},{4,20},{5,21},{6,22},{7,23},{8,24},{9,... | collective-permute-start | bytes 786440 | tf_op jit(solution)/shard_map/ppermute | solution.py:27
  46.1 1.0 %copy.7 = f32[1,1,512,512]{3,2,1,0:T(8,128)} copy(f32[1,1,512,512]{3,2,1,0:T(8,128)S(1)} %bitcast.5) | data formatting | bytes 2097152
  47.1 1.2 %shard_map.77 = (bf16[512,512]{1,0:T(8,128)(2,1)S(1)}, bf16[512,512]{1,0:T(8,128)(2,1)S(1)}) custom-call(s32[1,2]{1,0:T(1,128)S(1)} %copy-done, f32[512,512]{1,0:T(8,128)S(1)} %get-tuple-element.41.root_ref, bf16[512,512]{1,0:T(8,128)(2,1)S(1)} %get-tuple-element.44.high_ref, bf16[512,512]{1,0:T(8,128)(2,1)S(1)} %get-tuple-element.45.low_ref), custom_call_target="tpu_custom_call" | custom-call | tf_op jit(solution)/shard_map/pallas_call | solution.py:326
  48.3 8.8 %collective-permute-done.17 = f16[256,512]{1,0:T(8,128)(2,1)S(1)} collective-permute-done((f16[256,512]{1,0:T(8,128)(2,1)S(1)}, f16[256,512]{1,0:T(8,128)(2,1)S(1)}, u32[]{:S(2)}, u32[]{:S(2)}) %collective-permute-start.17) | collective-permute-done | bytes 262176 | tf_op jit(solution)/shard_map/ppermute | solution.py:27
  57.1 0.1 convert_element_type.61.got_ref
  57.2 0.1 convert_element_type.63.got_ref
  57.2 1.0 %shard_map.78 = (f32[256,512]{1,0:T(8,128)S(1)}, f32[8,512]{1,0:T(8,128)S(1)}) custom-call(s32[1,2]{1,0:T(1,128)S(1)} %copy-done, f32[264,512]{1,0:T(8,128)S(1)} %convert_element_type.63.got_ref, bf16[512,512]{1,0:T(8,128)(2,1)S(1)} %get-tuple-element.46.high_ref, bf16[512,512]{1,0:T(8,128)(2,1)S(1)} %get-tuple-element.47.low_ref), custom_call_target="tpu_custom_call" | custom-call | tf_op jit(solution)/shard_map/pallas_call | solution.py:326
  58.3 1.8 %shard_map.79 = f32[256,512]{1,0:T(8,128)} custom-call(s32[1,2]{1,0:T(1,128)S(1)} %copy-done, f32[256,512]{1,0:T(8,128)S(1)} %convert_element_type.61.got_ref, f32[8,512]{1,0:T(8,128)S(1)} %get-tuple-element.48.tail_ref, bf16[512,512]{1,0:T(8,128)(2,1)S(1)} %get-tuple-element.46.high_ref, bf16[512,512]{1,0:T(8,128)(2,1)S(1)} %get-tuple-element.47.low_ref, ...), custom_call_target="tpu_custom_call" | custom-call | tf_op jit(solution)/shard_map/pallas_call | solution.py:326
  (23 shorter events, 0.3 us)
Async XLA Ops:
  0.6 16.4 %collective-permute-start.2 = (bf16[1024,512]{1,0:T(8,128)(2,1)}, bf16[1024,512]{1,0:T(8,128)(2,1)S(1)}, u32[]{:S(2)}, u32[]{:S(2)}) collective-permute-start(bf16[1024,512]{1,0:T(8,128)(2,1)} %refs_1_.1), channel_id=1, source_target_pairs={{0,1},{1,0},{2,3},{3,2},{4,5},{5,4},{6,7},{7,6},{8,9},{9,8},{10,11... | collective-permute-start | bytes 3145736 | tf_op jit(solution)/shard_map/ppermute | solution.py:34
  1.2 7.8 %collective-permute-start.7 = (bf16[32,1024]{1,0:T(8,128)(2,1)}, bf16[32,1024]{1,0:T(8,128)(2,1)S(1)}, u32[]{:S(2)}, u32[]{:S(2)}) collective-permute-start(bf16[32,1024]{1,0:T(8,128)(2,1)} %bitcast.9), channel_id=1, source_target_pairs={{0,12},{1,13},{2,14},{3,15},{4,8},{5,9},{6,10},{7,11},{8,4},{9,5},... | collective-permute-start | bytes 196616 | tf_op jit(solution)/shard_map/ppermute | solution.py:34
  5.9 6.3 %collective-permute-start.6 = (bf16[32,1024]{1,0:T(8,128)(2,1)}, bf16[32,1024]{1,0:T(8,128)(2,1)S(1)}, u32[]{:S(2)}, u32[]{:S(2)}) collective-permute-start(bf16[32,1024]{1,0:T(8,128)(2,1)} %bitcast.10), channel_id=1, source_target_pairs={{0,8},{1,9},{2,10},{3,11},{4,12},{5,13},{6,14},{7,15},{8,0},{9,1},... | collective-permute-start | bytes 196616 | tf_op jit(solution)/shard_map/ppermute | solution.py:34
  5.9 7.8 %collective-permute-start.1 = (bf16[32,1024]{1,0:T(8,128)(2,1)}, bf16[32,1024]{1,0:T(8,128)(2,1)S(1)}, u32[]{:S(2)}, u32[]{:S(2)}) collective-permute-start(bf16[32,1024]{1,0:T(8,128)(2,1)} %bitcast.11), channel_id=1, source_target_pairs={{0,4},{1,5},{2,6},{3,7},{4,0},{5,1},{6,2},{7,3},{8,12},{9,13},{10,... | collective-permute-start | bytes 196616 | tf_op jit(solution)/shard_map/ppermute | solution.py:34
  9.0 6.8 %collective-permute-start.13 = (bf16[32,1024]{1,0:T(8,128)(2,1)S(1)}, bf16[32,1024]{1,0:T(8,128)(2,1)S(1)}, u32[]{:S(2)}, u32[]{:S(2)}) collective-permute-start(bf16[32,1024]{1,0:T(8,128)(2,1)S(1)} %collective-permute-done.7.refs_1_), channel_id=1, source_target_pairs={{0,2},{1,3},{2,0},{3,1},{4,6},{5,7},{6,4},{7,5},{8,10},{9,11},{10,... | collective-permute-start | bytes 196616 | tf_op jit(solution)/shard_map/ppermute | solution.py:34
  12.1 4.9 %collective-permute-start.12 = (bf16[32,1024]{1,0:T(8,128)(2,1)S(1)}, bf16[32,1024]{1,0:T(8,128)(2,1)S(1)}, u32[]{:S(2)}, u32[]{:S(2)}) collective-permute-start(bf16[32,1024]{1,0:T(8,128)(2,1)S(1)} %collective-permute-done.6.refs_0_), channel_id=1, source_target_pairs={{0,2},{1,3},{2,0},{3,1},{4,6},{5,7},{6,4},{7,5},{8,10},{9,11},{10,... | collective-permute-start | bytes 196616 | tf_op jit(solution)/shard_map/ppermute | solution.py:34
  13.6 5.7 %collective-permute-start.8 = (bf16[32,1024]{1,0:T(8,128)(2,1)S(1)}, bf16[32,1024]{1,0:T(8,128)(2,1)S(1)}, u32[]{:S(2)}, u32[]{:S(2)}) collective-permute-start(bf16[32,1024]{1,0:T(8,128)(2,1)S(1)} %collective-permute-done.1.refs_2_), channel_id=1, source_target_pairs={{0,2},{1,3},{2,0},{3,1},{4,6},{5,7},{6,4},{7,5},{8,10},{9,11},{10,... | collective-permute-start | bytes 196616 | tf_op jit(solution)/shard_map/ppermute | solution.py:34
  17.5 0.8 %copy-start.1 = (bf16[1024,32]{0,1:T(8,128)(2,1)S(1)}, bf16[1024,32]{0,1:T(8,128)(2,1)}, u32[]{:S(2)}) copy-start(bf16[1024,32]{0,1:T(8,128)(2,1)} %param.6) | copy-start | bytes 196612
  17.6 6.3 %collective-permute-start.16 = (f16[72,512]{1,0:T(8,128)(2,1)S(1)}, f16[72,512]{1,0:T(8,128)(2,1)S(1)}, u32[]{:S(2)}, u32[]{:S(2)}) collective-permute-start(f16[72,512]{1,0:T(8,128)(2,1)S(1)} %convert_element_type.58), channel_id=1, source_target_pairs={{0,17},{1,16},{2,19},{3,18},{4,21},{5,20},{6,23},{7,22},{8,25},{9,... | collective-permute-start | bytes 221192 | tf_op jit(solution)/shard_map/ppermute | solution.py:27
  18.4 4.9 %collective-permute-start = (bf16[32,1024]{1,0:T(8,128)(2,1)S(1)}, bf16[32,1024]{1,0:T(8,128)(2,1)S(1)}, u32[]{:S(2)}, u32[]{:S(2)}) collective-permute-start(bf16[32,1024]{1,0:T(8,128)(2,1)S(1)} %bitcast.13), channel_id=1, source_target_pairs={{0,2},{1,3},{2,0},{3,1},{4,6},{5,7},{6,4},{7,5},{8,10},{9,11},{10,... | collective-permute-start | bytes 196616 | tf_op jit(solution)/shard_map/ppermute | solution.py:34
  19.9 9.2 %collective-permute-start.11 = (f16[104,512]{1,0:T(8,128)(2,1)S(1)}, f16[104,512]{1,0:T(8,128)(2,1)S(1)}, u32[]{:S(2)}, u32[]{:S(2)}) collective-permute-start(f16[104,512]{1,0:T(8,128)(2,1)S(1)} %convert_element_type.54), channel_id=1, source_target_pairs={{0,17},{1,16},{2,19},{3,18},{4,21},{5,20},{6,23},{7,22},{8,25},{9,... | collective-permute-start | bytes 319496 | tf_op jit(solution)/shard_map/ppermute | solution.py:27
  20.7 9.7 %collective-permute-start.9 = (f16[104,512]{1,0:T(8,128)(2,1)S(1)}, f16[104,512]{1,0:T(8,128)(2,1)S(1)}, u32[]{:S(2)}, u32[]{:S(2)}) collective-permute-start(f16[104,512]{1,0:T(8,128)(2,1)S(1)} %convert_element_type.52), channel_id=1, source_target_pairs={{0,16},{1,17},{2,18},{3,19},{4,20},{5,21},{6,22},{7,23},{8,24},{9,... | collective-permute-start | bytes 319496 | tf_op jit(solution)/shard_map/ppermute | solution.py:27
  22.3 6.8 %collective-permute-start.14 = (f16[72,512]{1,0:T(8,128)(2,1)S(1)}, f16[72,512]{1,0:T(8,128)(2,1)S(1)}, u32[]{:S(2)}, u32[]{:S(2)}) collective-permute-start(f16[72,512]{1,0:T(8,128)(2,1)S(1)} %convert_element_type.56), channel_id=1, source_target_pairs={{0,16},{1,17},{2,18},{3,19},{4,20},{5,21},{6,22},{7,23},{8,24},{9,... | collective-permute-start | bytes 221192 | tf_op jit(solution)/shard_map/ppermute | solution.py:27
  23.8 13.1 %collective-permute-start.4 = (f32[96,512]{1,0:T(8,128)S(1)}, f32[96,512]{1,0:T(8,128)S(1)}, u32[]{:S(2)}, u32[]{:S(2)}) collective-permute-start(f32[96,512]{1,0:T(8,128)S(1)} %get-tuple-element.30), channel_id=1, source_target_pairs={{0,1},{1,0},{2,3},{3,2},{4,5},{5,4},{6,7},{7,6},{8,9},{9,8},{10,11... | collective-permute-start | bytes 589832 | tf_op jit(solution)/shard_map/ppermute | solution.py:34
  23.8 13.0 %collective-permute-start.10 = (f32[96,512]{1,0:T(8,128)S(1)}, f32[96,512]{1,0:T(8,128)S(1)}, u32[]{:S(2)}, u32[]{:S(2)}) collective-permute-start(f32[96,512]{1,0:T(8,128)S(1)} %get-tuple-element.34), channel_id=1, source_target_pairs={{0,1},{1,0},{2,3},{3,2},{4,5},{5,4},{6,7},{7,6},{8,9},{9,8},{10,11... | collective-permute-start | bytes 589832 | tf_op jit(solution)/shard_map/ppermute | solution.py:34
  29.1 7.7 %collective-permute-start.15 = (f32[64,512]{1,0:T(8,128)S(1)}, f32[64,512]{1,0:T(8,128)S(1)}, u32[]{:S(2)}, u32[]{:S(2)}) collective-permute-start(f32[64,512]{1,0:T(8,128)S(1)} %get-tuple-element.38), channel_id=1, source_target_pairs={{0,1},{1,0},{2,3},{3,2},{4,5},{5,4},{6,7},{7,6},{8,9},{9,8},{10,11... | collective-permute-start | bytes 393224 | tf_op jit(solution)/shard_map/ppermute | solution.py:34
  29.2 6.1 %collective-permute-start.5 = (f16[104,512]{1,0:T(8,128)(2,1)S(1)}, f16[104,512]{1,0:T(8,128)(2,1)S(1)}, u32[]{:S(2)}, u32[]{:S(2)}) collective-permute-start(f16[104,512]{1,0:T(8,128)(2,1)S(1)} %convert_element_type.50), channel_id=1, source_target_pairs={{0,17},{1,16},{2,19},{3,18},{4,21},{5,20},{6,23},{7,22},{8,25},{9,... | collective-permute-start | bytes 319496 | tf_op jit(solution)/shard_map/ppermute | solution.py:27
  30.4 6.3 %collective-permute-start.3 = (f16[104,512]{1,0:T(8,128)(2,1)S(1)}, f16[104,512]{1,0:T(8,128)(2,1)S(1)}, u32[]{:S(2)}, u32[]{:S(2)}) collective-permute-start(f16[104,512]{1,0:T(8,128)(2,1)S(1)} %convert_element_type.48), channel_id=1, source_target_pairs={{0,16},{1,17},{2,18},{3,19},{4,20},{5,21},{6,22},{7,23},{8,24},{9,... | collective-permute-start | bytes 319496 | tf_op jit(solution)/shard_map/ppermute | solution.py:27
  32.6 1.0 %copy-start = (s32[1,2]{1,0:T(1,128)S(1)}, s32[1,2]{1,0:T(1,128)}, u32[]{:S(2)}) copy-start(s32[1,2]{1,0:T(1,128)} %assign_ref.7) | copy-start | bytes 28
  43.9 13.2 %collective-permute-start.18 = (f16[264,512]{1,0:T(8,128)(2,1)S(1)}, f16[264,512]{1,0:T(8,128)(2,1)S(1)}, u32[]{:S(2)}, u32[]{:S(2)}) collective-permute-start(f16[264,512]{1,0:T(8,128)(2,1)S(1)} %convert_element_type.62), channel_id=1, source_target_pairs={{0,16},{1,17},{2,18},{3,19},{4,20},{5,21},{6,22},{7,23},{8,24},{9,... | collective-permute-start | bytes 811016 | tf_op jit(solution)/shard_map/ppermute | solution.py:27
  44.9 12.2 %collective-permute-start.17 = (f16[256,512]{1,0:T(8,128)(2,1)S(1)}, f16[256,512]{1,0:T(8,128)(2,1)S(1)}, u32[]{:S(2)}, u32[]{:S(2)}) collective-permute-start(f16[256,512]{1,0:T(8,128)(2,1)S(1)} %convert_element_type.60), channel_id=1, source_target_pairs={{0,16},{1,17},{2,18},{3,19},{4,20},{5,21},{6,22},{7,23},{8,24},{9,... | collective-permute-start | bytes 786440 | tf_op jit(solution)/shard_map/ppermute | solution.py:27
